TPU v7x, 32 devices: a whole 2x2x4 slice. The times are simulated.
32 devices in a mesh: ctx: 8 (over z, y), tp: 4 (over x, core).
Axes of the slice: x: 2, y: 2, z: 4, core: 2. Of those that a mesh axis runs over, the one named last changes fastest.
Arguments:
- queries: bfloat16 [4096, 4096], P('ctx', 'tp'), may hold values from -22 to 22
- keys: bfloat16 [4096, 512], P('ctx', 'tp'), may hold values from -22 to 22
- values: bfloat16 [4096, 512], P('ctx', 'tp'), may hold values from -36 to 36
- positions: int32 [3, 4096], P(None, 'ctx'), may hold values from 0 to 4095
- segment_ids: int32 [4096], replicated, may hold values from 0 to 3, never falling along the last dimension, each value on 1 to 2048 neighbouring positions
- out_weight: bfloat16 [4096, 8192], P('tp', 'ctx'), may hold values from -0.09375 to 0.09375
- residual: bfloat16 [4096, 8192], P(('ctx', 'tp')), may hold values from -3 to 3
Outputs:
- layer_out: bfloat16 [4096, 8192], P(('ctx', 'tp'))
Inputs may be any that keep to these rules, and one draw needn't show every extreme that they name: `segment_ids`: ids never fall along the sequence; each document has 1 to 2048 tokens, and one has exactly 2048.
All inputs are finite; a program needn't handle non-finite values.
Results may differ from a plain program's by a relative error of at most 0.013.
Values may be sent and summed in bfloat16 or wider, within the bound.
A program may use at most 128 MiB of HBM per device.

v0:
```python
import functools
import math

import jax
import jax.numpy as jnp
from jax import lax
from jax.experimental import pallas as pl
from jax.experimental.pallas import tpu as pltpu
from jax.sharding import PartitionSpec as P

HD = 128
DOC = 2048

theta_base = 1000000.0
MESH_ID = pl.DeviceIdType.MESH


def rotary_tables(positions):
    half_dim = HD // 2
    freq_index = jnp.arange(half_dim)
    inv_freq = theta_base ** (-2.0 * freq_index.astype(jnp.float32) / HD)
    first_end = HD // 8
    second_end = first_end + 3 * HD // 16
    place = positions.astype(jnp.float32)
    chosen = jnp.where(
        freq_index[None, :] < first_end,
        place[0][:, None],
        jnp.where(freq_index[None, :] < second_end, place[1][:, None], place[2][:, None]),
    )
    angle = chosen * inv_freq[None, :]
    return (jnp.cos(angle), jnp.sin(angle))


def rotate(vectors, cosine_table, sine_table):
    half_dim = HD // 2
    lower_half = vectors[..., :half_dim]
    upper_half = vectors[..., half_dim:]
    cos_b = cosine_table[:, None, :]
    sin_b = sine_table[:, None, :]
    return jnp.concatenate(
        [lower_half * cos_b - upper_half * sin_b, upper_half * cos_b + lower_half * sin_b], axis=-1
    )


def fused(
    n, inner, reach, tile,
    q_ref, kv_ref, start_ref, w_ref, out_ref,
    kvbuf, wbuf, abuf, bbuf, bias, xsend, xrecv, osend,
    kv_s, kv_r, w_s, w_r, up_s, down_s, a_r, f_s, b_r, x_s, x_r, o_s, o_r,
):
    outer = n // inner
    half = inner // 2
    tok = q_ref.shape[0]
    pairs = q_ref.shape[1] // (2 * HD)
    tiles = tok // tile
    span = reach * tok + tile
    rows = tok // 2
    quarter = rows // 2
    cols = w_ref.shape[1]
    c = lax.axis_index("ctx")
    t = lax.axis_index("tp")
    co, ci = c // inner, c % inner
    x, h = t // 2, t % 2
    other_x = 1 - x
    mate = {"ctx": c, "tp": 2 * x + 1 - h}
    across = {"ctx": c, "tp": 2 * other_x + h}

    def remote(src, dst, send, recv, device):
        return pltpu.make_async_remote_copy(
            src_ref=src, dst_ref=dst, send_sem=send, recv_sem=recv,
            device_id=device, device_id_type=MESH_ID,
        )

    def landed(dst, sem):
        pltpu.make_async_copy(dst, dst, sem).wait()

    barrier = pltpu.get_barrier_semaphore()

    def greet(device):
        pl.semaphore_signal(barrier, inc=1, device_id=device, device_id_type=MESH_ID)

    for d in range(1, reach + 1):
        @pl.when(c + d < n)
        def _():
            greet({"ctx": c + d, "tp": t})

        @pl.when(c >= d)
        def _():
            greet({"ctx": c - d, "tp": t})
    for d in range(1, inner):
        for g in range(2):
            greet({"ctx": co * inner + (ci + d) % inner, "tp": 2 * x + g})
    for d in range(1, outer):
        for g in range(2):
            greet({"ctx": (co + d) % outer * inner + ci, "tp": 2 * x + g})
    greet(mate)
    greet(across)
    near = jnp.minimum(reach, n - 1 - c) + jnp.minimum(reach, c)
    pl.semaphore_wait(barrier, near + 2 * (inner - 1) + 2 * (outer - 1) + 2)

    def kv_slot(d):
        return kvbuf.at[:, pl.ds((reach - d) * tok, tok), :]

    def kv_copy(d):
        return remote(kv_ref, kv_slot(d), kv_s.at[d - 1], kv_r.at[d - 1], {"ctx": c + d, "tp": t})

    for d in range(1, reach + 1):
        @pl.when(c + d < n)
        def _():
            kv_copy(d).start()

    owner = ci // half
    w_slot = wbuf.at[h, ci % half]
    w_sem = w_r.at[h, ci % half]

    def w_copy(d):
        device = {"ctx": co * inner + (ci + d) % inner, "tp": 2 * x + owner}
        return remote(w_ref, w_slot, w_s.at[d], w_sem, device)

    for d in range(1, inner):
        w_copy(d).start()

    @pl.when(owner != h)
    def _():
        w_copy(0).start()

    @pl.when(owner == h)
    def _():
        pltpu.make_async_copy(w_ref, w_slot, w_sem).start()

    kvbuf[:, reach * tok:, :] = kv_ref[...]
    for d in range(1, reach + 1):
        @pl.when(c < d)
        def _():
            kvbuf[:, (reach - d) * tok:(reach - d + 1) * tok, :] = jnp.zeros(kv_ref.shape, kv_ref.dtype)

    def fill_bias(rt, _):
        first = start_ref[pl.ds(pl.multiple_of(rt * tile, tile), tile), :] - (
            (c - reach) * tok + rt * tile
        )
        key = lax.broadcasted_iota(jnp.int32, (tile, span), 1)
        query = lax.broadcasted_iota(jnp.int32, (tile, span), 0) + reach * tok
        bias[rt] = jnp.where((key <= query) & (key >= first), 0.0, -1e30).astype(jnp.float32)
        return 0

    lax.fori_loop(0, tiles, fill_bias, 0)

    for d in range(1, reach + 1):
        @pl.when(c >= d)
        def _():
            landed(kv_slot(d), kv_r.at[d - 1])

    factor = math.log2(math.e) / math.sqrt(HD)

    def up_copy(slot, hp):
        device = {"ctx": c + inner, "tp": t}
        return remote(abuf.at[slot, hp], abuf.at[slot, hp], up_s.at[slot, hp], a_r.at[slot, hp], device)

    def down_copy(slot, hp):
        device = {"ctx": c - inner, "tp": t}
        return remote(abuf.at[slot, hp], abuf.at[slot, hp], down_s.at[slot, hp], a_r.at[slot, hp], device)

    def f_copy(slot, hp):
        return remote(abuf.at[slot, hp], bbuf.at[slot, hp], f_s.at[slot, hp], b_r.at[slot, hp], mate)

    def pass_on(slot, hp):
        @pl.when((slot <= co) & (co + 1 < outer))
        def _():
            up_copy(slot, hp).start()

        @pl.when((slot >= co) & (co >= 1))
        def _():
            down_copy(slot, hp).start()

        f_copy(slot, hp).start()

    def forward(slot, hp):
        landed(abuf.at[slot, hp], a_r.at[slot, hp])
        pass_on(slot, hp)

    def each_side(distance, action):
        def one_side(side, _):
            slot = co + distance * (2 * side - 1)

            @pl.when((slot >= 0) & (slot < outer) & ((distance > 0) | (side == 1)))
            def _():
                action(slot)
            return 0

        lax.fori_loop(0, 2, one_side, 0)

    def attend(hp, _):
        def one_tile(rt, _):
            at = pl.ds(pl.multiple_of(rt * tile, tile), tile)
            window = pl.ds(pl.multiple_of(rt * tile, tile), span)
            k = kvbuf[0, window, :]
            v = kvbuf[1, window, :]
            q2 = q_ref[at, pl.ds(pl.multiple_of(hp * 2 * HD, 2 * HD), 2 * HD)]
            done = []
            for e in range(2):
                q = q2[:, e * HD:(e + 1) * HD]
                s = lax.dot_general(
                    q, k, (((1,), (1,)), ((), ())), preferred_element_type=jnp.float32
                ) + bias[rt]
                peak = jnp.max(s, axis=-1, keepdims=True)
                p = jnp.exp2((s - peak) * factor)
                total = jnp.sum(p, axis=-1, keepdims=True)
                mixed = jnp.dot(p.astype(jnp.bfloat16), v, preferred_element_type=jnp.float32)
                done.append((mixed / total).astype(jnp.bfloat16))
            abuf[co, hp, at, :] = jnp.concatenate(done, axis=1)
            return 0

        lax.fori_loop(0, tiles, one_tile, 0)
        pass_on(co, hp)

        @pl.when(hp >= lag)
        def _():
            each_side(1, lambda slot: forward(slot, hp - lag))
        return 0

    lag = min(2, pairs)
    lax.fori_loop(0, pairs, attend, 0)

    for i in range(half):
        landed(wbuf.at[0, i], w_r.at[0, i])
        landed(wbuf.at[1, i], w_r.at[1, i])

    def x_copy(slot):
        return remote(xsend.at[slot], xrecv.at[slot], x_s.at[slot], x_r.at[slot], across)

    wide = out_ref.shape[1] // (2 * outer)

    def out_slot(slot, g):
        return out_ref.at[:, pl.ds(pl.multiple_of((slot * 2 + g) * wide, 128), wide)]

    def o_copy(slot, g):
        device = {"ctx": slot * inner + ci, "tp": 2 * x + g}
        return remote(osend.at[slot, g], out_slot(co, h), o_s.at[slot, g], o_r.at[co, h], device)

    def product(slot, side, i):
        at = pl.ds(pl.multiple_of(side * rows, rows), rows)
        mine = jnp.concatenate([abuf[slot, p, at, :] for p in range(pairs)], axis=1)
        theirs = jnp.concatenate([bbuf[slot, p, at, :] for p in range(pairs)], axis=1)
        return jnp.dot(mine, wbuf[h, i], preferred_element_type=jnp.float32) + jnp.dot(
            theirs, wbuf[1 - h, i], preferred_element_type=jnp.float32
        )

    def send_product(slot):
        def arrive(hp, _):
            landed(bbuf.at[slot, hp], b_r.at[slot, hp])
            return 0

        lax.fori_loop(0, pairs, arrive, 0)
        for i in range(half):
            xsend[slot, :, i * cols:(i + 1) * cols] = product(slot, other_x, i).astype(jnp.bfloat16)
        x_copy(slot).start()

    def add_product(slot):
        landed(xrecv.at[slot], x_r.at[slot])
        for i in range(half):
            at = slice(i * cols, (i + 1) * cols)
            both = (product(slot, x, i) + xrecv[slot, :, at].astype(jnp.float32)).astype(jnp.bfloat16)
            osend[slot, 0, :, at] = both[:quarter]
            osend[slot, 1, :, at] = both[quarter:]
        for g in range(2):
            @pl.when((slot != co) | (h != g))
            def _():
                o_copy(slot, g).start()

            @pl.when((slot == co) & (h == g))
            def _():
                out_ref[:, pl.ds(pl.multiple_of((co * 2 + h) * wide, 128), wide)] = osend[slot, g]

    def step(d, _):
        each_side(d - 1, send_product)

        def rest(slot):
            first = jnp.where(d == 1, pairs - lag, 0)

            def one(hp, _):
                forward(slot, hp)
                return 0

            lax.fori_loop(first, pairs, one, 0)

        each_side(d, rest)
        each_side(d - 1, add_product)
        return 0

    lax.fori_loop(1, outer + 1, step, 0)

    for d in range(1, reach + 1):
        @pl.when(c + d < n)
        def _():
            kv_copy(d).wait_send()
    for d in range(1, inner):
        w_copy(d).wait_send()

    @pl.when(owner != h)
    def _():
        w_copy(0).wait_send()

    def drain(slot, _):
        def sent(hp, _):
            f_copy(slot, hp).wait_send()

            @pl.when((slot <= co) & (co + 1 < outer))
            def _():
                up_copy(slot, hp).wait_send()

            @pl.when((slot >= co) & (co >= 1))
            def _():
                down_copy(slot, hp).wait_send()
            return 0

        lax.fori_loop(0, pairs, sent, 0)
        x_copy(slot).wait_send()
        for g in range(2):
            @pl.when((slot != co) | (h != g))
            def _():
                o_copy(slot, g).wait_send()
                landed(out_slot(slot, g), o_r.at[slot, g])
        return 0

    lax.fori_loop(0, outer, drain, 0)


def on_device(queries, keys, values, positions, segment_ids, out_weight, residual):
    tok = queries.shape[0]
    heads = queries.shape[1] // HD
    n = lax.axis_size("ctx")
    inner = 2 ** max(1, int(math.log2(n)) // 2)
    outer = n // inner
    half = inner // 2
    reach = (DOC + tok - 2) // tok
    tile = math.gcd(tok, 256)
    my_start = lax.axis_index("ctx") * tok
    depth, cols = out_weight.shape
    cosine_table, sine_table = rotary_tables(positions)
    rot_q = rotate(
        queries.reshape(tok, heads, HD).astype(jnp.float32), cosine_table, sine_table
    ).astype(jnp.bfloat16).reshape(tok, heads * HD)
    rot_k = rotate(
        keys.reshape(tok, 1, HD).astype(jnp.float32), cosine_table, sine_table
    ).astype(jnp.bfloat16).reshape(tok, HD)
    pair = jnp.stack([rot_k, values], axis=0)
    my_seg = lax.dynamic_slice_in_dim(segment_ids, my_start, tok, 0)
    start = jnp.sum((segment_ids[None, :] < my_seg[:, None]).astype(jnp.int32), axis=1, keepdims=True)
    pairs = heads // 2
    rows = tok // 2
    wide = half * cols
    bf16 = jnp.bfloat16
    dma = pltpu.SemaphoreType.DMA
    vmem = pl.BlockSpec(memory_space=pltpu.VMEM)
    gathered = pl.pallas_call(
        functools.partial(fused, n, inner, reach, tile),
        out_shape=jax.ShapeDtypeStruct((rows // 2, outer * 2 * wide), bf16),
        in_specs=[vmem] * 4,
        out_specs=vmem,
        scratch_shapes=[
            pltpu.VMEM((2, (reach + 1) * tok, HD), bf16),
            pltpu.VMEM((2, half, depth, cols), bf16),
            pltpu.VMEM((outer, pairs, tok, 2 * HD), bf16),
            pltpu.VMEM((outer, pairs, tok, 2 * HD), bf16),
            pltpu.VMEM((tok // tile, tile, reach * tok + tile), jnp.float32),
            pltpu.VMEM((outer, rows, wide), bf16),
            pltpu.VMEM((outer, rows, wide), bf16),
            pltpu.VMEM((outer, 2, rows // 2, wide), bf16),
            dma((reach,)), dma((reach,)),
            dma((inner,)), dma((2, half)),
            dma((outer, pairs)),
            dma((outer, pairs)), dma((outer, pairs)),
            dma((outer, pairs)), dma((outer, pairs)),
            dma((outer,)), dma((outer,)),
            dma((outer, 2)), dma((outer, 2)),
        ],
        compiler_params=pltpu.CompilerParams(
            collective_id=0, has_side_effects=True, vmem_limit_bytes=60 * 1024 * 1024
        ),
    )(rot_q, pair, start, out_weight)
    return (gathered.astype(jnp.float32) + residual.astype(jnp.float32)).astype(jnp.bfloat16)


def solution(mesh):
    return jax.shard_map(
        on_device,
        mesh=mesh,
        in_specs=(
            P("ctx", "tp"),
            P("ctx", "tp"),
            P("ctx", "tp"),
            P(None, "ctx"),
            P(),
            P("tp", "ctx"),
            P(("ctx", "tp"), None),
        ),
        out_specs=P(("ctx", "tp"), None),
        check_vma=False,
    )
```

profile of v0, /device:TPU:5, one launch (start us, length us, event | category | flops | bytes accessed | tf_op | source)
XLA Modules:
  0.0 160.5 jit_solution(17442838525612214493)
XLA Ops:
  0.0 0.7 convert_element_type.53
  0.7 1.7 %fusion.3 = (f32[512,64]{1,0:T(8,128)S(1)}, f32[512,64]{1,0:T(8,128)S(1)}) fusion(f32[64]{0:T(128)S(1)} %multiply_power_fusion, f32[512]{0:T(512)S(1)} %bitcast.25, f32[512]{0:T(512)S(1)} %bitcast.27, f32[512]{0:T(512)S(1)} %bitcast.23, pred[64]{0:T(512)(128)(4,1)S(1)} %get-tuple-element.14, pred[64]{0:T(512)(128)(4,1)S(1)} %get-tuple-element.15), kind=kLoop, calls=%fused_computation.15 | loop fusion | flops 98304 | bytes 268672 | tf_op jit(solution)/shard_map/cos | solution.py:31
  2.4 1.5 convert_bitcast_fusion
  3.9 0.5 copy.10
  4.4 0.8 subtract_convert_fusion
  5.2 0.0 copy-start.1
  5.2 0.6 pad_maximum_fusion
  5.8 0.0 copy-start.2
  5.8 0.0 copy-start.3
  5.8 1.2 copy.13
  7.1 0.0 copy-done.1
  7.1 1.4 fusion.4
  8.5 0.0 copy-done.2
  8.5 0.8 pad_maximum_fusion.1.kv_ref
  9.3 0.0 copy-done.3
  9.3 0.1 dynamic_slice.3
  9.4 1.0 convert_reduce_fusion
  10.4 0.9 copy.9.start_ref
  11.3 0.0 copy-start
  11.3 145.8 %shard_map.73 = bf16[128,8192]{1,0:T(8,128)(2,1)} custom-call(bf16[512,1024]{1,0:T(8,128)(2,1)} %bitcast.21, bf16[2,512,128]{2,1,0:T(8,128)(2,1)} %pad_maximum_fusion.1.kv_ref, s32[512,1]{1,0:T(8,128)} %copy.9.start_ref, bf16[1024,1024]{1,0:T(8,128)(2,1)} %w_ref.1), custom_call_target="tpu_custom_call" | custom-call | tf_op jit(solution)/shard_map/pallas_call | solution.py:355
  157.1 0.0 copy-done
  157.1 3.4 %add_convert_fusion = bf16[128,8192]{1,0:T(8,128)(2,1)} fusion(bf16[128,8192]{1,0:T(8,128)(2,1)S(1)} %copy-done, bf16[128,8192]{1,0:T(8,128)(2,1)} %shard_map.73), kind=kLoop, calls=%fused_computation.1 | loop fusion | flops 4194304 | bytes 6291456 | tf_op jit(solution)/shard_map/convert_element_type | solution.py:381
  (4 shorter events, 0.0 us)
Async XLA Ops:
  5.2 1.9 %copy-start.1 = (bf16[512,128]{1,0:T(8,128)(2,1)S(1)}, bf16[512,128]{1,0:T(8,128)(2,1)}, u32[]{:S(2)}) copy-start(bf16[512,128]{1,0:T(8,128)(2,1)} %param.8) | copy-start | bytes 393220
  5.8 2.7 %copy-start.2 = (bf16[512,128]{1,0:T(8,128)(2,1)S(1)}, bf16[512,128]{1,0:T(8,128)(2,1)}, u32[]{:S(2)}) copy-start(bf16[512,128]{1,0:T(8,128)(2,1)} %param.9) | copy-start | bytes 393220
  5.8 3.5 %copy-start.3 = (s32[4096]{0:T(1024)S(1)}, s32[4096]{0:T(1024)}, u32[]{:S(2)}) copy-start(s32[4096]{0:T(1024)} %param.11) | copy-start | bytes 49156
  11.3 145.8 %copy-start = (bf16[128,8192]{1,0:T(8,128)(2,1)S(1)}, bf16[128,8192]{1,0:T(8,128)(2,1)}, u32[]{:S(2)}) copy-start(bf16[128,8192]{1,0:T(8,128)(2,1)} %param.13) | copy-start | bytes 6291460
where the time goes:
time: 161 us; the launch traced here: 160 us
  Pallas kernels  146 us (91%)
  other arithmetic  11.9 us (7%)
  local copies, waits for them, and re-layouts  2.7 us (2%)
    pallas_call x1, Pallas kernels, on_device(): pl.pallas_call(functools.partial(fused, n, inner, reach, tile), out_shape...  146 us
    convert_element_type x1, other arithmetic, on_device(): (gathered.astype(jnp.float32) + residual.astype(jnp.float32)).astype(jnp....  3.41 us

commit v1 on v0

v1 whole, which is shorter than its diff:
```python
import functools
import math

import jax
import jax.numpy as jnp
from jax import lax
from jax.experimental import pallas as pl
from jax.experimental.pallas import tpu as pltpu
from jax.sharding import PartitionSpec as P

HD = 128
DOC = 2048

theta_base = 1000000.0
MESH_ID = pl.DeviceIdType.MESH


def rotary_tables(positions):
    half_dim = HD // 2
    freq_index = jnp.arange(half_dim)
    inv_freq = theta_base ** (-2.0 * freq_index.astype(jnp.float32) / HD)
    first_end = HD // 8
    second_end = first_end + 3 * HD // 16
    place = positions.astype(jnp.float32)
    chosen = jnp.where(
        freq_index[None, :] < first_end,
        place[0][:, None],
        jnp.where(freq_index[None, :] < second_end, place[1][:, None], place[2][:, None]),
    )
    angle = chosen * inv_freq[None, :]
    return (jnp.cos(angle), jnp.sin(angle))


def rotate(vectors, cosine_table, sine_table):
    half_dim = HD // 2
    lower_half = vectors[..., :half_dim]
    upper_half = vectors[..., half_dim:]
    cos_b = cosine_table[:, None, :]
    sin_b = sine_table[:, None, :]
    return jnp.concatenate(
        [lower_half * cos_b - upper_half * sin_b, upper_half * cos_b + lower_half * sin_b], axis=-1
    )


def fused(
    n, inner, reach, tile,
    q_ref, kv_ref, start_ref, w_ref, out_ref,
    kvbuf, wbuf, att, abuf, bias, pbuf, hbuf, xrecv, obuf,
    kv_s, kv_r, w_r, wu_s, wd_s, wm_s, a_s, a_r, ha_s, ha_r, x_s, x_r, p_s, p_r, o_s, o_r,
):
    outer = n // inner
    tok = q_ref.shape[0]
    pairs = q_ref.shape[1] // (2 * HD)
    tiles = tok // tile
    span = reach * tok + tile
    quarter = tok // 4
    pieces, cut = wbuf.shape[2], wbuf.shape[4]
    cols = w_ref.shape[1]
    block = inner * quarter
    chained = reach % inner == 0
    c = lax.axis_index("ctx")
    t = lax.axis_index("tp")
    co, ci = c // inner, c % inner
    x, h = t // 2, t % 2
    other_x = 1 - x
    last = outer - 1
    is_end = (co == 0) | (co == last)
    helps = (co == 1) | (co == last - 1)
    helped = jnp.where(co == 1, 0, last)
    helper = jnp.where(co == 0, 1, last - 1)
    mate = {"ctx": c, "tp": 2 * x + 1 - h}
    across = {"ctx": c, "tp": 2 * other_x + h}

    def remote(src, dst, send, recv, device):
        return pltpu.make_async_remote_copy(
            src_ref=src, dst_ref=dst, send_sem=send, recv_sem=recv,
            device_id=device, device_id_type=MESH_ID,
        )

    def landed(dst, sem):
        pltpu.make_async_copy(dst, dst, sem).wait()

    def own_piece(j):
        return pltpu.make_async_copy(
            w_ref.at[:, j * cut:(j + 1) * cut], wbuf.at[co, h, j], w_r.at[co, h, j]
        )

    for j in range(pieces):
        own_piece(j).start()

    barrier = pltpu.get_barrier_semaphore()

    def greet(device):
        pl.semaphore_signal(barrier, inc=1, device_id=device, device_id_type=MESH_ID)

    for k in range(inner):
        near = (ci + k) % inner
        for g in range(2):
            if k + g > 0:
                greet({"ctx": co * inner + near, "tp": 2 * x + (h + g) % 2})

            @pl.when(co < last)
            def _():
                greet({"ctx": (co + 1) * inner + near, "tp": 2 * x + g})

            @pl.when(co > 0)
            def _():
                greet({"ctx": (co - 1) * inner + near, "tp": 2 * x + g})
    greet(across)
    beside = jnp.where(co < last, 1, 0) + jnp.where(co > 0, 1, 0)
    pl.semaphore_wait(barrier, 2 * inner + 2 * inner * beside)

    def kv_slot(d):
        start = (reach - d) * tok
        if not isinstance(d, int):
            start = pl.multiple_of(start, tok)
        return kvbuf.at[:, pl.ds(start, tok), :]

    def kv_sends(s, action):
        src = kv_ref if s == 0 else kv_slot(s * inner)

        def one(k, slot, device):
            action(remote(src, kv_slot(slot), kv_s.at[s, k], kv_r.at[slot - 1], device))

        if not chained:
            for d in range(1, reach + 1):
                @pl.when(c + d < n)
                def _():
                    one(d, d, {"ctx": c + d, "tp": t})
            return

        @pl.when(co >= s)
        def _():
            if (s + 1) * inner <= reach:
                @pl.when(co < last)
                def _():
                    one(0, (s + 1) * inner, {"ctx": c + inner, "tp": t})
            for k in range(1, inner):
                near = (ci + k) % inner
                away = s * inner + near - ci

                @pl.when((away >= 1) & (away <= reach))
                def _():
                    one(k, away, {"ctx": co * inner + near, "tp": t})

    stages = reach // inner + 1 if chained else 1
    kv_sends(0, lambda copy: copy.start())

    def w_up(slot, j):
        device = {"ctx": c + inner, "tp": t}
        return remote(wbuf.at[slot, h, j], wbuf.at[slot, h, j], wu_s.at[slot, j], w_r.at[slot, h, j], device)

    def w_down(slot, j):
        device = {"ctx": c - inner, "tp": t}
        return remote(wbuf.at[slot, h, j], wbuf.at[slot, h, j], wd_s.at[slot, j], w_r.at[slot, h, j], device)

    def w_mate(slot, j):
        return remote(wbuf.at[slot, h, j], wbuf.at[slot, h, j], wm_s.at[slot, j], w_r.at[slot, h, j], mate)

    def goes_up(slot):
        return (slot <= co) & (co < last) & ((co + 1 < last) | (slot == co))

    def goes_down(slot):
        return (slot >= co) & (co > 0) & ((co > 1) | (slot == co))

    def has(slot):
        return jnp.logical_not(is_end) | ((slot - co <= 1) & (co - slot <= 1))

    def pass_on(slot, j):
        @pl.when(goes_up(slot))
        def _():
            w_up(slot, j).start()

        @pl.when(goes_down(slot))
        def _():
            w_down(slot, j).start()

        w_mate(slot, j).start()

    early = min(2, pieces)
    own_piece(0).wait()
    pass_on(co, 0)

    kvbuf[:, reach * tok:, :] = kv_ref[...]
    for d in range(1, reach + 1):
        @pl.when(c < d)
        def _():
            kvbuf[:, (reach - d) * tok:(reach - d + 1) * tok, :] = jnp.zeros(kv_ref.shape, kv_ref.dtype)

    def fill_bias(rt, _):
        first = start_ref[pl.ds(pl.multiple_of(rt * tile, tile), tile), :] - (
            (c - reach) * tok + rt * tile
        )
        key = lax.broadcasted_iota(jnp.int32, (tile, span), 1)
        query = lax.broadcasted_iota(jnp.int32, (tile, span), 0) + reach * tok
        bias[rt] = jnp.where((key <= query) & (key >= first), 0.0, -1e30).astype(jnp.float32)
        return 0

    lax.fori_loop(0, tiles, fill_bias, 0)

    for s in range(1, stages):
        @pl.when(co >= s)
        def _():
            landed(kv_slot(s * inner), kv_r.at[s * inner - 1])

        kv_sends(s, lambda copy: copy.start())

    for j in range(1, pieces):
        own_piece(j).wait()
        if j < early:
            pass_on(co, j)
        else:
            @pl.when(jnp.logical_not(is_end))
            def _():
                pass_on(co, j)

    for d in range(1, reach + 1):
        if not chained or d % inner != 0:
            @pl.when(c >= d)
            def _():
                landed(kv_slot(d), kv_r.at[d - 1])

    factor = math.log2(math.e) / math.sqrt(HD)

    def rows_of(side, at):
        return pl.ds(pl.multiple_of((side * inner + at) * quarter, quarter), quarter)

    def a_copies(hp, action):
        lanes = pl.ds(pl.multiple_of(hp * 2 * HD, 2 * HD), 2 * HD)
        for side in range(2):
            for k in range(inner):
                near = (ci + k) % inner
                for gg in range(2):
                    g = (h + gg) % 2
                    src = att.at[pl.ds(pl.multiple_of((2 * side + g) * quarter, quarter), quarter), lanes]
                    if k + gg > 0:
                        action(remote(
                            src, abuf.at[0, h, rows_of(side, ci), lanes], a_s.at[k, gg],
                            a_r.at[ci, h, side], {"ctx": co * inner + near, "tp": 2 * x + g},
                        ))

                    @pl.when(is_end)
                    def _():
                        action(remote(
                            src, abuf.at[1, h, rows_of(side, ci), lanes], ha_s.at[k, gg],
                            ha_r.at[ci, h, side], {"ctx": helper * inner + near, "tp": 2 * x + g},
                        ))

    def attend(hp, _):
        lanes = pl.ds(pl.multiple_of(hp * 2 * HD, 2 * HD), 2 * HD)

        def one_tile(rt, _):
            at = pl.ds(pl.multiple_of(rt * tile, tile), tile)
            window = pl.ds(pl.multiple_of(rt * tile, tile), span)
            k = kvbuf[0, window, :]
            v = kvbuf[1, window, :]
            q2 = q_ref[at, lanes]
            done = []
            for e in range(2):
                q = q2[:, e * HD:(e + 1) * HD]
                s = lax.dot_general(
                    q, k, (((1,), (1,)), ((), ())), preferred_element_type=jnp.float32
                ) + bias[rt]
                peak = jnp.max(s, axis=-1, keepdims=True)
                p = jnp.exp2((s - peak) * factor)
                total = jnp.sum(p, axis=-1, keepdims=True)
                mixed = jnp.dot(p.astype(jnp.bfloat16), v, preferred_element_type=jnp.float32)
                done.append((mixed / total).astype(jnp.bfloat16))
            att[at, lanes] = jnp.concatenate(done, axis=1)
            return 0

        lax.fori_loop(0, tiles, one_tile, 0)
        a_copies(hp, lambda copy: copy.start())
        for side in range(2):
            src = pl.ds(pl.multiple_of((2 * side + h) * quarter, quarter), quarter)
            abuf[0, h, rows_of(side, ci), lanes] = att[src, lanes]
        return 0

    lax.fori_loop(0, pairs, attend, 0)

    @pl.when(is_end)
    def _():
        for j in range(early, pieces):
            pass_on(co, j)

    for k in range(inner):
        near = (ci + k) % inner
        for gg in range(2):
            if k + gg > 0:
                g = (h + gg) % 2
                for side in range(2):
                    landed(abuf.at[0, g, rows_of(side, near), :], a_r.at[near, g, side])

    def x_copy(slot, j):
        return remote(pbuf.at[slot, j, other_x], xrecv.at[slot, j], x_s.at[slot, j], x_r.at[slot, j], across)

    def p_copy(slot, j):
        device = {"ctx": helped * inner + ci, "tp": t}
        return remote(hbuf.at[slot, j], pbuf.at[slot, j], p_s.at[slot, j], p_r.at[slot, j], device)

    def out_slot(slot, j, at):
        return out_ref.at[:, pl.ds(pl.multiple_of((slot * inner + at) * cols + j * cut, 128), cut)]

    def o_copy(slot, j, k):
        near = (ci + k) % inner
        device = {"ctx": co * inner + near, "tp": t}
        return remote(obuf.at[slot, j, near], out_slot(slot, j, ci), o_s.at[slot, j, k], o_r.at[slot, j, ci], device)

    def product(who, slot, j, into):
        for side in range(2):
            at = slice(side * block, (side + 1) * block)
            into[slot, j, side] = (
                jnp.dot(abuf[who, 0, at, :], wbuf[slot, 0, j], preferred_element_type=jnp.float32)
                + jnp.dot(abuf[who, 1, at, :], wbuf[slot, 1, j], preferred_element_type=jnp.float32)
            ).astype(jnp.bfloat16)

    def lends(slot):
        return helps & (slot != helped) & (slot != co)

    def send_product(d, slot, j):
        @pl.when(has(slot))
        def _():
            @pl.when(d > 0)
            def _():
                landed(wbuf.at[slot, h, j], w_r.at[slot, h, j])
                pass_on(slot, j)

            landed(wbuf.at[slot, 1 - h, j], w_r.at[slot, 1 - h, j])

            @pl.when(lends(slot))
            def _():
                product(1, slot, j, hbuf)
                p_copy(slot, j).start()

            product(0, slot, j, pbuf)

        @pl.when(jnp.logical_not(has(slot)))
        def _():
            landed(pbuf.at[slot, j], p_r.at[slot, j])

        x_copy(slot, j).start()

    def add_product(slot, j):
        landed(xrecv.at[slot, j], x_r.at[slot, j])
        both = (
            pbuf[slot, j, x].astype(jnp.float32) + xrecv[slot, j].astype(jnp.float32)
        ).astype(jnp.bfloat16)
        for k in range(inner):
            obuf[slot, j, k] = both[k * quarter:(k + 1) * quarter]
        for k in range(1, inner):
            o_copy(slot, j, k).start()
        out_ref[:, pl.ds(pl.multiple_of((slot * inner + ci) * cols + j * cut, 128), cut)] = obuf[slot, j, ci]

    def each_side(distance, action):
        def one_side(side, _):
            slot = co + distance * (2 * side - 1)

            @pl.when((slot >= 0) & (slot < outer) & ((distance > 0) | (side == 1)))
            def _():
                action(slot)
            return 0

        lax.fori_loop(0, 2, one_side, 0)

    def first_unit(j, _):
        send_product(0, co, j)
        return 0

    lax.fori_loop(0, pieces, first_unit, 0)

    @pl.when(helps)
    def _():
        for k in range(inner):
            for g in range(2):
                for side in range(2):
                    landed(abuf.at[1, g, rows_of(side, k), :], ha_r.at[k, g, side])

    def step(i, _):
        d, j = i // pieces, i % pieces

        @pl.when(d < outer)
        def _():
            each_side(d, lambda slot: send_product(d, slot, j))

        before = i - pieces
        each_side(before // pieces, lambda slot: add_product(slot, before % pieces))
        return 0

    lax.fori_loop(pieces, (outer + 1) * pieces, step, 0)

    for s in range(stages):
        kv_sends(s, lambda copy: copy.wait_send())
    for k in range(inner):
        for gg in range(2):
            if k + gg > 0:
                landed(abuf.at[0, 0, 0:2 * quarter, :], a_s.at[k, gg])

            @pl.when(is_end)
            def _():
                landed(abuf.at[0, 0, 0:2 * quarter, :], ha_s.at[k, gg])

    def drain(i, _):
        slot, j = i // pieces, i % pieces

        @pl.when(has(slot))
        def _():
            w_mate(slot, j).wait_send()

            @pl.when(goes_up(slot))
            def _():
                w_up(slot, j).wait_send()

            @pl.when(goes_down(slot))
            def _():
                w_down(slot, j).wait_send()

        @pl.when(lends(slot))
        def _():
            p_copy(slot, j).wait_send()

        x_copy(slot, j).wait_send()
        for k in range(1, inner):
            o_copy(slot, j, k).wait_send()
            near = (ci + k) % inner
            landed(out_slot(slot, j, near), o_r.at[slot, j, near])
        return 0

    lax.fori_loop(0, outer * pieces, drain, 0)


def on_device(queries, keys, values, positions, segment_ids, out_weight, residual):
    tok = queries.shape[0]
    heads = queries.shape[1] // HD
    n = lax.axis_size("ctx")
    inner = 2 ** max(1, int(math.log2(n)) // 2)
    outer = n // inner
    reach = (DOC + tok - 2) // tok
    tile = math.gcd(tok, 256)
    my_start = lax.axis_index("ctx") * tok
    depth, cols = out_weight.shape
    cut = math.gcd(cols, 256)
    pieces = cols // cut
    cosine_table, sine_table = rotary_tables(positions)
    rot_q = rotate(
        queries.reshape(tok, heads, HD).astype(jnp.float32), cosine_table, sine_table
    ).astype(jnp.bfloat16).reshape(tok, heads * HD)
    rot_k = rotate(
        keys.reshape(tok, 1, HD).astype(jnp.float32), cosine_table, sine_table
    ).astype(jnp.bfloat16).reshape(tok, HD)
    pair = jnp.stack([rot_k, values], axis=0)
    my_seg = lax.dynamic_slice_in_dim(segment_ids, my_start, tok, 0)
    start = jnp.sum((segment_ids[None, :] < my_seg[:, None]).astype(jnp.int32), axis=1, keepdims=True)
    quarter = tok // 4
    block = inner * quarter
    bf16 = jnp.bfloat16
    dma = pltpu.SemaphoreType.DMA
    vmem = pl.BlockSpec(memory_space=pltpu.VMEM)
    gathered = pl.pallas_call(
        functools.partial(fused, n, inner, reach, tile),
        out_shape=jax.ShapeDtypeStruct((quarter, n * cols), bf16),
        in_specs=[vmem] * 3 + [pl.BlockSpec(memory_space=pl.ANY)],
        out_specs=vmem,
        scratch_shapes=[
            pltpu.VMEM((2, (reach + 1) * tok, HD), bf16),
            pltpu.VMEM((outer, 2, pieces, depth, cut), bf16),
            pltpu.VMEM((tok, depth), bf16),
            pltpu.VMEM((2, 2, 2 * block, depth), bf16),
            pltpu.VMEM((tok // tile, tile, reach * tok + tile), jnp.float32),
            pltpu.VMEM((outer, pieces, 2, block, cut), bf16),
            pltpu.VMEM((outer, pieces, 2, block, cut), bf16),
            pltpu.VMEM((outer, pieces, block, cut), bf16),
            pltpu.VMEM((outer, pieces, inner, quarter, cut), bf16),
            dma((reach + 1, max(inner, reach + 1))), dma((reach,)),
            dma((outer, 2, pieces)),
            dma((outer, pieces)), dma((outer, pieces)), dma((outer, pieces)),
            dma((inner, 2)), dma((inner, 2, 2)),
            dma((inner, 2)), dma((inner, 2, 2)),
            dma((outer, pieces)), dma((outer, pieces)),
            dma((outer, pieces)), dma((outer, pieces)),
            dma((outer, pieces, inner)), dma((outer, pieces, inner)),
        ],
        compiler_params=pltpu.CompilerParams(
            collective_id=0, has_side_effects=True, vmem_limit_bytes=60 * 1024 * 1024
        ),
    )(rot_q, pair, start, out_weight)
    return (gathered.astype(jnp.float32) + residual.astype(jnp.float32)).astype(jnp.bfloat16)


def solution(mesh):
    return jax.shard_map(
        on_device,
        mesh=mesh,
        in_specs=(
            P("ctx", "tp"),
            P("ctx", "tp"),
            P("ctx", "tp"),
            P(None, "ctx"),
            P(),
            P("tp", "ctx"),
            P(("ctx", "tp"), None),
        ),
        out_specs=P(("ctx", "tp"), None),
        check_vma=False,
    )
```

time: 161 us -> 176 us (1.093)
  the two profiles are of different devices: /device:TPU:5 before, /device:TPU:0 now
where the time goes in v1:
time: 176 us
  Pallas kernels  161 us (91%)
  other arithmetic  11.9 us (7%)
  local copies, waits for them, and re-layouts  2.7 us (2%)
    pallas_call x1, Pallas kernels, on_device(): pl.pallas_call(functools.partial(fused, n, inner, reach, tile), out_shape...  161 us

profile of v1, /device:TPU:0, one launch (start us, length us, event | category | flops | bytes accessed | tf_op | source)
XLA Modules:
  0.0 175.7 jit_solution(11253039980485880215)
XLA Ops:
  0.0 0.7 convert_element_type.53
  0.7 1.7 fusion.3
  2.4 1.5 convert_bitcast_fusion
  3.9 0.5 copy.10
  4.4 0.8 subtract_convert_fusion
  5.2 0.0 copy-start.1
  5.2 0.6 pad_maximum_fusion
  5.8 0.0 copy-start.2
  5.8 0.0 copy-start.3
  5.8 1.2 copy.13
  7.1 0.0 copy-done.1
  7.1 1.4 fusion.4
  8.5 0.0 copy-done.2
  8.5 0.8 pad_maximum_fusion.1.kv_ref
  9.3 0.0 copy-done.3
  9.3 0.1 dynamic_slice.3
  9.4 1.0 convert_reduce_fusion
  10.4 0.9 copy.9.start_ref
  11.3 0.0 copy-start
  11.3 161.0 %shard_map.73 = bf16[128,8192]{1,0:T(8,128)(2,1)} custom-call(bf16[512,1024]{1,0:T(8,128)(2,1)} %bitcast.21, bf16[2,512,128]{2,1,0:T(8,128)(2,1)} %pad_maximum_fusion.1.kv_ref, s32[512,1]{1,0:T(8,128)} %copy.9.start_ref, bf16[1024,1024]{1,0:T(8,128)(2,1)} %w_ref.1), custom_call_target="tpu_custom_call" | custom-call | tf_op jit(solution)/shard_map/pallas_call | solution.py:458
  172.3 0.0 copy-done
  172.3 3.4 %add_convert_fusion = bf16[128,8192]{1,0:T(8,128)(2,1)} fusion(bf16[128,8192]{1,0:T(8,128)(2,1)S(1)} %copy-done, bf16[128,8192]{1,0:T(8,128)(2,1)} %shard_map.73), kind=kLoop, calls=%fused_computation.1 | loop fusion | flops 4194304 | bytes 6291456 | tf_op jit(solution)/shard_map/convert_element_type | solution.py:486
  (4 shorter events, 0.0 us)
Async XLA Ops:
  5.2 1.9 %copy-start.1 = (bf16[512,128]{1,0:T(8,128)(2,1)S(1)}, bf16[512,128]{1,0:T(8,128)(2,1)}, u32[]{:S(2)}) copy-start(bf16[512,128]{1,0:T(8,128)(2,1)} %param.8) | copy-start | bytes 393220
  5.8 2.7 %copy-start.2 = (bf16[512,128]{1,0:T(8,128)(2,1)S(1)}, bf16[512,128]{1,0:T(8,128)(2,1)}, u32[]{:S(2)}) copy-start(bf16[512,128]{1,0:T(8,128)(2,1)} %param.9) | copy-start | bytes 393220
  5.8 3.5 %copy-start.3 = (s32[4096]{0:T(1024)S(1)}, s32[4096]{0:T(1024)}, u32[]{:S(2)}) copy-start(s32[4096]{0:T(1024)} %param.11) | copy-start | bytes 49156
  11.3 161.0 %copy-start = (bf16[128,8192]{1,0:T(8,128)(2,1)S(1)}, bf16[128,8192]{1,0:T(8,128)(2,1)}, u32[]{:S(2)}) copy-start(bf16[128,8192]{1,0:T(8,128)(2,1)} %param.13) | copy-start | bytes 6291460

commit v2 on v1

--- a/solution.py
+++ b/solution.py
@@ -45,8 +45,8 @@
 def fused(
     n, inner, reach, tile,
     q_ref, kv_ref, start_ref, w_ref, out_ref,
-    kvbuf, wbuf, att, abuf, bias, pbuf, hbuf, xrecv, obuf,
-    kv_s, kv_r, w_r, wu_s, wd_s, wm_s, a_s, a_r, ha_s, ha_r, x_s, x_r, p_s, p_r, o_s, o_r,
+    kvbuf, wbuf, att, abuf, bias, pbuf, xrecv, obuf,
+    kv_s, kv_r, w_r, wu_s, wd_s, wm_s, a_s, a_r, ha_s, hf_s, ha_r, x_s, x_r, o_s, o_r,
 ):
     outer = n // inner
     tok = q_ref.shape[0]
@@ -110,17 +110,18 @@
     beside = jnp.where(co < last, 1, 0) + jnp.where(co > 0, 1, 0)
     pl.semaphore_wait(barrier, 2 * inner + 2 * inner * beside)
 
-    def kv_slot(d):
-        start = (reach - d) * tok
-        if not isinstance(d, int):
-            start = pl.multiple_of(start, tok)
-        return kvbuf.at[:, pl.ds(start, tok), :]
-
-    def kv_sends(s, action):
-        src = kv_ref if s == 0 else kv_slot(s * inner)
+    half = tok // 2
+    kv_parts = 4
+
+    def kv_slot(d, part):
+        start = pl.multiple_of((reach - d) * tok + part % 2 * half, half)
+        return kvbuf.at[part // 2, pl.ds(start, half), :]
+
+    def kv_sends(s, part, action):
+        src = kv_ref.at[part // 2, pl.ds(part % 2 * half, half), :] if s == 0 else kv_slot(s * inner, part)
 
         def one(k, slot, device):
-            action(remote(src, kv_slot(slot), kv_s.at[s, k], kv_r.at[slot - 1], device))
+            action(remote(src, kv_slot(slot, part), kv_s.at[s, k, part], kv_r.at[slot - 1, part], device))
 
         if not chained:
             for d in range(1, reach + 1):
@@ -144,7 +145,11 @@
                     one(k, away, {"ctx": co * inner + near, "tp": t})
 
     stages = reach // inner + 1 if chained else 1
-    kv_sends(0, lambda copy: copy.start())
+    for part in range(kv_parts):
+        kv_sends(0, part, lambda copy: copy.start())
+
+    early = min(2, pieces)
+    shared = pieces // 2
 
     def w_up(slot, j):
         device = {"ctx": c + inner, "tp": t}
@@ -157,29 +162,54 @@
     def w_mate(slot, j):
         return remote(wbuf.at[slot, h, j], wbuf.at[slot, h, j], wm_s.at[slot, j], w_r.at[slot, h, j], mate)
 
-    def goes_up(slot):
-        return (slot <= co) & (co < last) & ((co + 1 < last) | (slot == co))
-
-    def goes_down(slot):
-        return (slot >= co) & (co > 0) & ((co > 1) | (slot == co))
-
-    def has(slot):
-        return jnp.logical_not(is_end) | ((slot - co <= 1) & (co - slot <= 1))
-
-    def pass_on(slot, j):
-        @pl.when(goes_up(slot))
+    def near_end(away, j):
+        return (away <= 1) | ((away == 2) & (j < shared))
+
+    def goes_up(slot, j):
+        return (slot <= co) & (co < last) & ((co + 1 < last) | near_end(co + 1 - slot, j))
+
+    def goes_down(slot, j):
+        return (slot >= co) & (co > 0) & ((co > 1) | near_end(slot - co + 1, j))
+
+    def has(slot, j):
+        return jnp.logical_not(is_end) | (near_end(slot - co, j) & near_end(co - slot, j))
+
+    def lends(slot, j):
+        away = jnp.where(slot < helped, helped - slot, slot - helped)
+        return helps & jnp.logical_not(near_end(away, j))
+
+    def pass_up(slot, j):
+        @pl.when(goes_up(slot, j))
         def _():
             w_up(slot, j).start()
 
-        @pl.when(goes_down(slot))
+    def pass_down(slot, j):
+        @pl.when(goes_down(slot, j))
         def _():
             w_down(slot, j).start()
 
-        w_mate(slot, j).start()
-
-    early = min(2, pieces)
-    own_piece(0).wait()
-    pass_on(co, 0)
+    def own_up():
+        for j in range(pieces):
+            if j < early:
+                pass_up(co, j)
+            else:
+                @pl.when(jnp.logical_not(is_end))
+                def _():
+                    pass_up(co, j)
+
+    for j in range(pieces):
+        own_piece(j).wait()
+        if j < early:
+            pass_down(co, j)
+        else:
+            @pl.when(jnp.logical_not(is_end))
+            def _():
+                pass_down(co, j)
+        w_mate(co, j).start()
+
+    @pl.when(co == 0)
+    def _():
+        own_up()
 
     kvbuf[:, reach * tok:, :] = kv_ref[...]
     for d in range(1, reach + 1):
@@ -199,26 +229,28 @@
     lax.fori_loop(0, tiles, fill_bias, 0)
 
     for s in range(1, stages):
-        @pl.when(co >= s)
-        def _():
-            landed(kv_slot(s * inner), kv_r.at[s * inner - 1])
-
-        kv_sends(s, lambda copy: copy.start())
-
-    for j in range(1, pieces):
-        own_piece(j).wait()
-        if j < early:
-            pass_on(co, j)
-        else:
-            @pl.when(jnp.logical_not(is_end))
-            def _():
-                pass_on(co, j)
+        for part in range(kv_parts):
+            @pl.when(co >= s)
+            def _():
+                landed(kv_slot(s * inner, part), kv_r.at[s * inner - 1, part])
+
+            kv_sends(s, part, lambda copy: copy.start())
+        if s == 1:
+            @pl.when(co > 0)
+            def _():
+                own_up()
+
+    if stages == 1:
+        @pl.when(co > 0)
+        def _():
+            own_up()
 
     for d in range(1, reach + 1):
         if not chained or d % inner != 0:
             @pl.when(c >= d)
             def _():
-                landed(kv_slot(d), kv_r.at[d - 1])
+                for part in range(kv_parts):
+                    landed(kv_slot(d, part), kv_r.at[d - 1, part])
 
     factor = math.log2(math.e) / math.sqrt(HD)
 
@@ -239,12 +271,13 @@
                             a_r.at[ci, h, side], {"ctx": co * inner + near, "tp": 2 * x + g},
                         ))
 
-                    @pl.when(is_end)
-                    def _():
-                        action(remote(
-                            src, abuf.at[1, h, rows_of(side, ci), lanes], ha_s.at[k, gg],
-                            ha_r.at[ci, h, side], {"ctx": helper * inner + near, "tp": 2 * x + g},
-                        ))
+                    if k == 0:
+                        @pl.when(is_end)
+                        def _():
+                            action(remote(
+                                src, abuf.at[1, h, rows_of(side, ci), lanes], ha_s.at[gg],
+                                ha_r.at[ci, h, side], {"ctx": helper * inner + ci, "tp": 2 * x + g},
+                            ))
 
     def attend(hp, _):
         lanes = pl.ds(pl.multiple_of(hp * 2 * HD, 2 * HD), 2 * HD)
@@ -278,10 +311,36 @@
 
     lax.fori_loop(0, pairs, attend, 0)
 
+    def each_side(distance, j, action):
+        def one_side(side, _):
+            slot = co + distance * (2 * side - 1)
+
+            @pl.when((slot >= 0) & (slot < outer) & ((distance > 0) | (side == 1)))
+            def _():
+                @pl.when(has(slot, j))
+                def _():
+                    action(slot)
+            return 0
+
+        lax.fori_loop(0, 2, one_side, 0)
+
+    def arrive(slot, j):
+        landed(wbuf.at[slot, h, j], w_r.at[slot, h, j])
+        pass_up(slot, j)
+        pass_down(slot, j)
+        w_mate(slot, j).start()
+
+    def whole(slot, j):
+        landed(wbuf.at[slot, 1 - h, j], w_r.at[slot, 1 - h, j])
+
     @pl.when(is_end)
     def _():
         for j in range(early, pieces):
-            pass_on(co, j)
+            pass_up(co, j)
+            pass_down(co, j)
+
+    for j in range(early):
+        each_side(1, j, lambda slot: arrive(slot, j))
 
     for k in range(inner):
         near = (ci + k) % inner
@@ -291,138 +350,175 @@
                 for side in range(2):
                     landed(abuf.at[0, g, rows_of(side, near), :], a_r.at[near, g, side])
 
-    def x_copy(slot, j):
-        return remote(pbuf.at[slot, j, other_x], xrecv.at[slot, j], x_s.at[slot, j], x_r.at[slot, j], across)
-
-    def p_copy(slot, j):
-        device = {"ctx": helped * inner + ci, "tp": t}
-        return remote(hbuf.at[slot, j], pbuf.at[slot, j], p_s.at[slot, j], p_r.at[slot, j], device)
+    def x_copy(who, slot, j):
+        return remote(
+            pbuf.at[who, slot, j, other_x], xrecv.at[who, slot, j],
+            x_s.at[who, slot, j], x_r.at[who, slot, j], across,
+        )
 
     def out_slot(slot, j, at):
         return out_ref.at[:, pl.ds(pl.multiple_of((slot * inner + at) * cols + j * cut, 128), cut)]
 
-    def o_copy(slot, j, k):
+    def o_copy(who, slot, j, k):
         near = (ci + k) % inner
-        device = {"ctx": co * inner + near, "tp": t}
-        return remote(obuf.at[slot, j, near], out_slot(slot, j, ci), o_s.at[slot, j, k], o_r.at[slot, j, ci], device)
-
-    def product(who, slot, j, into):
+        node = helped if who else co
+        device = {"ctx": node * inner + near, "tp": t}
+        return remote(
+            obuf.at[who, slot, j, near], out_slot(slot, j, ci),
+            o_s.at[who, slot, j, k], o_r.at[slot, j, ci], device,
+        )
+
+    def job(who, slot, j):
         for side in range(2):
             at = slice(side * block, (side + 1) * block)
-            into[slot, j, side] = (
+            pbuf[who, slot, j, side] = (
                 jnp.dot(abuf[who, 0, at, :], wbuf[slot, 0, j], preferred_element_type=jnp.float32)
                 + jnp.dot(abuf[who, 1, at, :], wbuf[slot, 1, j], preferred_element_type=jnp.float32)
             ).astype(jnp.bfloat16)
-
-    def lends(slot):
-        return helps & (slot != helped) & (slot != co)
-
-    def send_product(d, slot, j):
-        @pl.when(has(slot))
-        def _():
-            @pl.when(d > 0)
-            def _():
-                landed(wbuf.at[slot, h, j], w_r.at[slot, h, j])
-                pass_on(slot, j)
-
-            landed(wbuf.at[slot, 1 - h, j], w_r.at[slot, 1 - h, j])
-
-            @pl.when(lends(slot))
-            def _():
-                product(1, slot, j, hbuf)
-                p_copy(slot, j).start()
-
-            product(0, slot, j, pbuf)
-
-        @pl.when(jnp.logical_not(has(slot)))
-        def _():
-            landed(pbuf.at[slot, j], p_r.at[slot, j])
-
-        x_copy(slot, j).start()
-
-    def add_product(slot, j):
-        landed(xrecv.at[slot, j], x_r.at[slot, j])
+        x_copy(who, slot, j).start()
+
+    def finish(who, slot, j):
+        landed(xrecv.at[who, slot, j], x_r.at[who, slot, j])
         both = (
-            pbuf[slot, j, x].astype(jnp.float32) + xrecv[slot, j].astype(jnp.float32)
+            pbuf[who, slot, j, x].astype(jnp.float32) + xrecv[who, slot, j].astype(jnp.float32)
         ).astype(jnp.bfloat16)
         for k in range(inner):
-            obuf[slot, j, k] = both[k * quarter:(k + 1) * quarter]
+            obuf[who, slot, j, k] = both[k * quarter:(k + 1) * quarter]
+        for k in range(1 - who, inner):
+            o_copy(who, slot, j, k).start()
+        if not who:
+            out_ref[:, pl.ds(pl.multiple_of((slot * inner + ci) * cols + j * cut, 128), cut)] = obuf[who, slot, j, ci]
+
+    beyond = 2 * co - helped
+
+    def forwards(action):
         for k in range(1, inner):
-            o_copy(slot, j, k).start()
-        out_ref[:, pl.ds(pl.multiple_of((slot * inner + ci) * cols + j * cut, 128), cut)] = obuf[slot, j, ci]
-
-    def each_side(distance, action):
-        def one_side(side, _):
-            slot = co + distance * (2 * side - 1)
-
-            @pl.when((slot >= 0) & (slot < outer) & ((distance > 0) | (side == 1)))
-            def _():
-                action(slot)
-            return 0
-
-        lax.fori_loop(0, 2, one_side, 0)
-
-    def first_unit(j, _):
-        send_product(0, co, j)
-        return 0
-
-    lax.fori_loop(0, pieces, first_unit, 0)
-
-    @pl.when(helps)
-    def _():
-        for k in range(inner):
+            near = (ci + k) % inner
             for g in range(2):
                 for side in range(2):
-                    landed(abuf.at[1, g, rows_of(side, k), :], ha_r.at[k, g, side])
+                    here = abuf.at[1, g, rows_of(side, ci), :]
+                    action(remote(
+                        here, here, hf_s.at[k, g, side], ha_r.at[ci, g, side],
+                        {"ctx": co * inner + near, "tp": t},
+                    ))
 
     def step(i, _):
         d, j = i // pieces, i % pieces
 
+        @pl.when((d > 1) & (d < outer))
+        def _():
+            each_side(d, j, lambda slot: arrive(slot, j))
+
+        @pl.when(helps & (i == 1))
+        def _():
+            for g in range(2):
+                for side in range(2):
+                    landed(abuf.at[1, g, rows_of(side, ci), :], ha_r.at[ci, g, side])
+            forwards(lambda copy: copy.start())
+
+        @pl.when(helps & (i == 2 * pieces))
+        def _():
+            for k in range(1, inner):
+                near = (ci + k) % inner
+                for g in range(2):
+                    for side in range(2):
+                        landed(abuf.at[1, g, rows_of(side, near), :], ha_r.at[near, g, side])
+
+            def lend(jj, _):
+                job(1, beyond, jj)
+                return 0
+
+            lax.fori_loop(shared, pieces, lend, 0)
+
+        def begins(slot):
+            whole(slot, j)
+
+            @pl.when(lends(slot, j) & (d > 1))
+            def _():
+                job(1, slot, j)
+
+            job(0, slot, j)
+
         @pl.when(d < outer)
         def _():
-            each_side(d, lambda slot: send_product(d, slot, j))
-
-        before = i - pieces
-        each_side(before // pieces, lambda slot: add_product(slot, before % pieces))
+            each_side(d, j, begins)
+
+        before = i - lag
+        then = before % pieces
+
+        @pl.when(before >= 0)
+        def _():
+            def ends(slot):
+                @pl.when(lends(slot, then) & (before >= 2 * pieces))
+                def _():
+                    finish(1, slot, then)
+
+                finish(0, slot, then)
+
+            each_side(before // pieces, then, ends)
+
+        @pl.when(helps & (d == 2) & (j >= shared))
+        def _():
+            finish(1, beyond, j)
+
+        @pl.when((d == 1) & (j + early < pieces))
+        def _():
+            each_side(1, j, lambda slot: arrive(slot, j + early))
         return 0
 
-    lax.fori_loop(pieces, (outer + 1) * pieces, step, 0)
+    lag = 3
+    lax.fori_loop(0, outer * pieces + lag, step, 0)
 
     for s in range(stages):
-        kv_sends(s, lambda copy: copy.wait_send())
+        for part in range(kv_parts):
+            kv_sends(s, part, lambda copy: copy.wait_send())
     for k in range(inner):
         for gg in range(2):
             if k + gg > 0:
                 landed(abuf.at[0, 0, 0:2 * quarter, :], a_s.at[k, gg])
 
-            @pl.when(is_end)
-            def _():
-                landed(abuf.at[0, 0, 0:2 * quarter, :], ha_s.at[k, gg])
+    @pl.when(is_end)
+    def _():
+        for gg in range(2):
+            landed(abuf.at[0, 0, 0:2 * quarter, :], ha_s.at[gg])
+
+    @pl.when(helps)
+    def _():
+        forwards(lambda copy: copy.wait_send())
 
     def drain(i, _):
         slot, j = i // pieces, i % pieces
 
-        @pl.when(has(slot))
+        @pl.when(has(slot, j))
         def _():
             w_mate(slot, j).wait_send()
 
-            @pl.when(goes_up(slot))
+            @pl.when(goes_up(slot, j))
             def _():
                 w_up(slot, j).wait_send()
 
-            @pl.when(goes_down(slot))
+            @pl.when(goes_down(slot, j))
             def _():
                 w_down(slot, j).wait_send()
 
-        @pl.when(lends(slot))
-        def _():
-            p_copy(slot, j).wait_send()
-
-        x_copy(slot, j).wait_send()
-        for k in range(1, inner):
-            o_copy(slot, j, k).wait_send()
+            x_copy(0, slot, j).wait_send()
+            for k in range(1, inner):
+                o_copy(0, slot, j, k).wait_send()
+
+        @pl.when(lends(slot, j))
+        def _():
+            x_copy(1, slot, j).wait_send()
+            for k in range(inner):
+                o_copy(1, slot, j, k).wait_send()
+
+        for k in range(inner):
             near = (ci + k) % inner
-            landed(out_slot(slot, j, near), o_r.at[slot, j, near])
+            if k == 0:
+                @pl.when(jnp.logical_not(has(slot, j)))
+                def _():
+                    landed(out_slot(slot, j, near), o_r.at[slot, j, near])
+            else:
+                landed(out_slot(slot, j, near), o_r.at[slot, j, near])
         return 0
 
     lax.fori_loop(0, outer * pieces, drain, 0)
@@ -466,18 +562,16 @@
             pltpu.VMEM((tok, depth), bf16),
             pltpu.VMEM((2, 2, 2 * block, depth), bf16),
             pltpu.VMEM((tok // tile, tile, reach * tok + tile), jnp.float32),
-            pltpu.VMEM((outer, pieces, 2, block, cut), bf16),
-            pltpu.VMEM((outer, pieces, 2, block, cut), bf16),
-            pltpu.VMEM((outer, pieces, block, cut), bf16),
-            pltpu.VMEM((outer, pieces, inner, quarter, cut), bf16),
-            dma((reach + 1, max(inner, reach + 1))), dma((reach,)),
+            pltpu.VMEM((2, outer, pieces, 2, block, cut), bf16),
+            pltpu.VMEM((2, outer, pieces, block, cut), bf16),
+            pltpu.VMEM((2, outer, pieces, inner, quarter, cut), bf16),
+            dma((reach + 1, max(inner, reach + 1), 4)), dma((reach, 4)),
             dma((outer, 2, pieces)),
             dma((outer, pieces)), dma((outer, pieces)), dma((outer, pieces)),
             dma((inner, 2)), dma((inner, 2, 2)),
-            dma((inner, 2)), dma((inner, 2, 2)),
-            dma((outer, pieces)), dma((outer, pieces)),
-            dma((outer, pieces)), dma((outer, pieces)),
-            dma((outer, pieces, inner)), dma((outer, pieces, inner)),
+            dma((2,)), dma((inner, 2, 2)), dma((inner, 2, 2)),
+            dma((2, outer, pieces)), dma((2, outer, pieces)),
+            dma((2, outer, pieces, inner)), dma((outer, pieces, inner)),
         ],
         compiler_params=pltpu.CompilerParams(
             collective_id=0, has_side_effects=True, vmem_limit_bytes=60 * 1024 * 1024

time: 176 us -> 145 us (0.82)
  Pallas kernels: 161 us -> 130 us
    pallas_call x1, Pallas kernels: 161 us -> 130 us  [on_device(): pl.pallas_call(functools.partial(fused, n, inner, reach, tile), out_shape...]
where the time goes in v2:
time: 145 us; the launch traced here: 144 us
  Pallas kernels  130 us (90%)
  other arithmetic  11.9 us (8%)
  local copies, waits for them, and re-layouts  2.7 us (2%)
    pallas_call x1, Pallas kernels, on_device(): pl.pallas_call(functools.partial(fused, n, inner, reach, tile), out_shape...  130 us
    convert_element_type x1, other arithmetic, on_device(): (gathered.astype(jnp.float32) + residual.astype(jnp.float32)).astype(jnp....  3.41 us

profile of v2, /device:TPU:0, one launch (start us, length us, event | category | flops | bytes accessed | tf_op | source)
XLA Modules:
  0.0 144.3 jit_solution(8927172708729868789)
XLA Ops:
  0.0 0.7 convert_element_type.53
  0.7 1.7 %fusion.3 = (f32[512,64]{1,0:T(8,128)S(1)}, f32[512,64]{1,0:T(8,128)S(1)}) fusion(f32[64]{0:T(128)S(1)} %multiply_power_fusion, f32[512]{0:T(512)S(1)} %bitcast.25, f32[512]{0:T(512)S(1)} %bitcast.27, f32[512]{0:T(512)S(1)} %bitcast.23, pred[64]{0:T(512)(128)(4,1)S(1)} %get-tuple-element.14, pred[64]{0:T(512)(128)(4,1)S(1)} %get-tuple-element.15), kind=kLoop, calls=%fused_computation.15 | loop fusion | flops 98304 | bytes 268672 | tf_op jit(solution)/shard_map/cos | solution.py:31
  2.4 1.5 %convert_bitcast_fusion = f32[64,8,8,128]{3,1,2,0:T(8,128)S(1)} fusion(bf16[512,1024]{1,0:T(8,128)(2,1)} %param.7), kind=kLoop, calls=%fused_computation.2 | loop fusion | flops 524288 | bytes 3145728
  3.9 0.5 copy.10
  4.4 0.8 subtract_convert_fusion
  5.2 0.0 copy-start.1
  5.2 0.6 pad_maximum_fusion
  5.8 0.0 copy-start.2
  5.8 0.0 copy-start.3
  5.8 1.2 copy.13
  7.1 0.0 copy-done.1
  7.1 1.4 fusion.4
  8.5 0.0 copy-done.2
  8.5 0.8 pad_maximum_fusion.1.kv_ref
  9.3 0.0 copy-done.3
  9.3 0.1 dynamic_slice.3
  9.4 1.0 convert_reduce_fusion
  10.4 0.9 copy.9.start_ref
  11.3 0.0 copy-start
  11.3 129.6 %shard_map.73 = bf16[128,8192]{1,0:T(8,128)(2,1)} custom-call(bf16[512,1024]{1,0:T(8,128)(2,1)} %bitcast.21, bf16[2,512,128]{2,1,0:T(8,128)(2,1)} %pad_maximum_fusion.1.kv_ref, s32[512,1]{1,0:T(8,128)} %copy.9.start_ref, bf16[1024,1024]{1,0:T(8,128)(2,1)} %w_ref.1), custom_call_target="tpu_custom_call" | custom-call | tf_op jit(solution)/shard_map/pallas_call | solution.py:554
  140.8 0.0 copy-done
  140.9 3.4 %add_convert_fusion = bf16[128,8192]{1,0:T(8,128)(2,1)} fusion(bf16[128,8192]{1,0:T(8,128)(2,1)S(1)} %copy-done, bf16[128,8192]{1,0:T(8,128)(2,1)} %shard_map.73), kind=kLoop, calls=%fused_computation.1 | loop fusion | flops 4194304 | bytes 6291456 | tf_op jit(solution)/shard_map/convert_element_type | solution.py:580
  (4 shorter events, 0.0 us)
Async XLA Ops:
  5.2 1.9 %copy-start.1 = (bf16[512,128]{1,0:T(8,128)(2,1)S(1)}, bf16[512,128]{1,0:T(8,128)(2,1)}, u32[]{:S(2)}) copy-start(bf16[512,128]{1,0:T(8,128)(2,1)} %param.8) | copy-start | bytes 393220
  5.8 2.7 %copy-start.2 = (bf16[512,128]{1,0:T(8,128)(2,1)S(1)}, bf16[512,128]{1,0:T(8,128)(2,1)}, u32[]{:S(2)}) copy-start(bf16[512,128]{1,0:T(8,128)(2,1)} %param.9) | copy-start | bytes 393220
  5.8 3.5 %copy-start.3 = (s32[4096]{0:T(1024)S(1)}, s32[4096]{0:T(1024)}, u32[]{:S(2)}) copy-start(s32[4096]{0:T(1024)} %param.11) | copy-start | bytes 49156
  11.3 129.6 %copy-start = (bf16[128,8192]{1,0:T(8,128)(2,1)S(1)}, bf16[128,8192]{1,0:T(8,128)(2,1)}, u32[]{:S(2)}) copy-start(bf16[128,8192]{1,0:T(8,128)(2,1)} %param.13) | copy-start | bytes 6291460

commit v3 on v2

--- a/solution.py
+++ b/solution.py
@@ -3,6 +3,7 @@
 
 import jax
 import jax.numpy as jnp
+import numpy as np
 from jax import lax
 from jax.experimental import pallas as pl
 from jax.experimental.pallas import tpu as pltpu
@@ -15,37 +16,15 @@
 MESH_ID = pl.DeviceIdType.MESH
 
 
-def rotary_tables(positions):
-    half_dim = HD // 2
-    freq_index = jnp.arange(half_dim)
-    inv_freq = theta_base ** (-2.0 * freq_index.astype(jnp.float32) / HD)
-    first_end = HD // 8
-    second_end = first_end + 3 * HD // 16
-    place = positions.astype(jnp.float32)
-    chosen = jnp.where(
-        freq_index[None, :] < first_end,
-        place[0][:, None],
-        jnp.where(freq_index[None, :] < second_end, place[1][:, None], place[2][:, None]),
-    )
-    angle = chosen * inv_freq[None, :]
-    return (jnp.cos(angle), jnp.sin(angle))
-
-
-def rotate(vectors, cosine_table, sine_table):
-    half_dim = HD // 2
-    lower_half = vectors[..., :half_dim]
-    upper_half = vectors[..., half_dim:]
-    cos_b = cosine_table[:, None, :]
-    sin_b = sine_table[:, None, :]
-    return jnp.concatenate(
-        [lower_half * cos_b - upper_half * sin_b, upper_half * cos_b + lower_half * sin_b], axis=-1
-    )
+def half_frequencies():
+    index = np.arange(HD // 2, dtype=np.float64)
+    return np.power(theta_base, -2.0 * index / HD).astype(np.float32)[:, None]
 
 
 def fused(
     n, inner, reach, tile,
-    q_ref, kv_ref, start_ref, w_ref, out_ref,
-    kvbuf, wbuf, att, abuf, bias, pbuf, xrecv, obuf,
+    q_ref, k_ref, v_ref, place_ref, segment_ref, freq_ref, w_ref, out_ref,
+    cosine, sine, my_segment, segments, kvbuf, wbuf, att, abuf, bias, pbuf, xrecv, obuf,
     kv_s, kv_r, w_r, wu_s, wd_s, wm_s, a_s, a_r, ha_s, hf_s, ha_r, x_s, x_r, o_s, o_r,
 ):
     outer = n // inner
@@ -108,6 +87,25 @@
                 greet({"ctx": (co - 1) * inner + near, "tp": 2 * x + g})
     greet(across)
     beside = jnp.where(co < last, 1, 0) + jnp.where(co > 0, 1, 0)
+
+    def turned(vectors, at):
+        wide = vectors.astype(jnp.float32)
+        return (wide * cosine[at, :] + pltpu.roll(wide, HD // 2, 1) * sine[at, :]).astype(jnp.bfloat16)
+
+    everything = pl.ds(0, tok)
+    frequency = lax.broadcasted_iota(jnp.int32, (HD // 2, tok), 0)
+    place = place_ref[...].astype(jnp.float32)
+    first_end = HD // 8
+    second_end = first_end + 3 * HD // 16
+    chosen = jnp.where(
+        frequency < first_end, place[0:1], jnp.where(frequency < second_end, place[1:2], place[2:3])
+    )
+    angle = chosen * freq_ref[...]
+    cos_part, sin_part = jnp.cos(angle), jnp.sin(angle)
+    cosine[...] = jnp.concatenate([cos_part, cos_part], axis=0).T
+    sine[...] = jnp.concatenate([-sin_part, sin_part], axis=0).T
+    kvbuf[0, reach * tok:, :] = turned(k_ref[...], everything)
+    kvbuf[1, reach * tok:, :] = v_ref[...]
     pl.semaphore_wait(barrier, 2 * inner + 2 * inner * beside)
 
     half = tok // 2
@@ -118,7 +116,9 @@
         return kvbuf.at[part // 2, pl.ds(start, half), :]
 
     def kv_sends(s, part, action):
-        src = kv_ref.at[part // 2, pl.ds(part % 2 * half, half), :] if s == 0 else kv_slot(s * inner, part)
+        src = kv_slot(s * inner, part)
+        if s == 0 and part // 2 == 1:
+            src = v_ref.at[pl.ds(part % 2 * half, half), :]
 
         def one(k, slot, device):
             action(remote(src, kv_slot(slot, part), kv_s.at[s, k, part], kv_r.at[slot - 1, part], device))
@@ -148,7 +148,7 @@
     for part in range(kv_parts):
         kv_sends(0, part, lambda copy: copy.start())
 
-    early = min(2, pieces)
+    early = (pieces + 1) // 2
     shared = pieces // 2
 
     def w_up(slot, j):
@@ -211,19 +211,26 @@
     def _():
         own_up()
 
-    kvbuf[:, reach * tok:, :] = kv_ref[...]
-    for d in range(1, reach + 1):
+    for d in range(reach + 1):
         @pl.when(c < d)
         def _():
-            kvbuf[:, (reach - d) * tok:(reach - d + 1) * tok, :] = jnp.zeros(kv_ref.shape, kv_ref.dtype)
+            kvbuf[:, (reach - d) * tok:(reach - d + 1) * tok, :] = jnp.zeros((2, tok, HD), kvbuf.dtype)
+            segments[:, (reach - d) * tok:(reach - d + 1) * tok] = jnp.full((1, tok), -1, jnp.int32)
+
+        @pl.when(c >= d)
+        def _():
+            from_at = pl.multiple_of((c - d) * tok, tok)
+            segments[:, (reach - d) * tok:(reach - d + 1) * tok] = segment_ref[:, pl.ds(from_at, tok)]
+    own_ids = segments[:, reach * tok:].astype(jnp.float32)
+    my_segment[...] = jnp.broadcast_to(own_ids, (HD, tok)).T
 
     def fill_bias(rt, _):
-        first = start_ref[pl.ds(pl.multiple_of(rt * tile, tile), tile), :] - (
-            (c - reach) * tok + rt * tile
-        )
+        at = pl.ds(pl.multiple_of(rt * tile, tile), tile)
+        window = pl.ds(pl.multiple_of(rt * tile, tile), span)
+        same = my_segment[at, 0:1] == segments[:, window].astype(jnp.float32)
         key = lax.broadcasted_iota(jnp.int32, (tile, span), 1)
         query = lax.broadcasted_iota(jnp.int32, (tile, span), 0) + reach * tok
-        bias[rt] = jnp.where((key <= query) & (key >= first), 0.0, -1e30).astype(jnp.float32)
+        bias[rt] = jnp.where((key <= query) & same, 0.0, -1e30).astype(jnp.float32)
         return 0
 
     lax.fori_loop(0, tiles, fill_bias, 0)
@@ -290,7 +297,7 @@
             q2 = q_ref[at, lanes]
             done = []
             for e in range(2):
-                q = q2[:, e * HD:(e + 1) * HD]
+                q = turned(q2[:, e * HD:(e + 1) * HD], at)
                 s = lax.dot_general(
                     q, k, (((1,), (1,)), ((), ())), preferred_element_type=jnp.float32
                 ) + bias[rt]
@@ -466,7 +473,7 @@
             each_side(1, j, lambda slot: arrive(slot, j + early))
         return 0
 
-    lag = 3
+    lag = min(5, pieces + 2)
     lax.fori_loop(0, outer * pieces + lag, step, 0)
 
     for s in range(stages):
@@ -526,26 +533,14 @@
 
 def on_device(queries, keys, values, positions, segment_ids, out_weight, residual):
     tok = queries.shape[0]
-    heads = queries.shape[1] // HD
     n = lax.axis_size("ctx")
     inner = 2 ** max(1, int(math.log2(n)) // 2)
     outer = n // inner
     reach = (DOC + tok - 2) // tok
     tile = math.gcd(tok, 256)
-    my_start = lax.axis_index("ctx") * tok
     depth, cols = out_weight.shape
-    cut = math.gcd(cols, 256)
+    cut = math.gcd(cols, 128)
     pieces = cols // cut
-    cosine_table, sine_table = rotary_tables(positions)
-    rot_q = rotate(
-        queries.reshape(tok, heads, HD).astype(jnp.float32), cosine_table, sine_table
-    ).astype(jnp.bfloat16).reshape(tok, heads * HD)
-    rot_k = rotate(
-        keys.reshape(tok, 1, HD).astype(jnp.float32), cosine_table, sine_table
-    ).astype(jnp.bfloat16).reshape(tok, HD)
-    pair = jnp.stack([rot_k, values], axis=0)
-    my_seg = lax.dynamic_slice_in_dim(segment_ids, my_start, tok, 0)
-    start = jnp.sum((segment_ids[None, :] < my_seg[:, None]).astype(jnp.int32), axis=1, keepdims=True)
     quarter = tok // 4
     block = inner * quarter
     bf16 = jnp.bfloat16
@@ -554,9 +549,13 @@
     gathered = pl.pallas_call(
         functools.partial(fused, n, inner, reach, tile),
         out_shape=jax.ShapeDtypeStruct((quarter, n * cols), bf16),
-        in_specs=[vmem] * 3 + [pl.BlockSpec(memory_space=pl.ANY)],
+        in_specs=[vmem] * 6 + [pl.BlockSpec(memory_space=pl.ANY)],
         out_specs=vmem,
         scratch_shapes=[
+            pltpu.VMEM((tok, HD), jnp.float32),
+            pltpu.VMEM((tok, HD), jnp.float32),
+            pltpu.VMEM((tok, HD), jnp.float32),
+            pltpu.VMEM((1, (reach + 1) * tok), jnp.int32),
             pltpu.VMEM((2, (reach + 1) * tok, HD), bf16),
             pltpu.VMEM((outer, 2, pieces, depth, cut), bf16),
             pltpu.VMEM((tok, depth), bf16),
@@ -576,7 +575,7 @@
         compiler_params=pltpu.CompilerParams(
             collective_id=0, has_side_effects=True, vmem_limit_bytes=60 * 1024 * 1024
         ),
-    )(rot_q, pair, start, out_weight)
+    )(queries, keys, values, positions, segment_ids[None, :], half_frequencies(), out_weight)
     return (gathered.astype(jnp.float32) + residual.astype(jnp.float32)).astype(jnp.bfloat16)
 
 

time: 145 us -> 136 us (0.938)
  other arithmetic: 11.9 us -> 3.41 us
  local copies, waits for them, and re-layouts: 2.7 us -> 0.01 us
  Pallas kernels: 130 us -> 132 us
    pallas_call x1, Pallas kernels: 130 us -> 132 us  [on_device(): pl.pallas_call(functools.partial(fused, n, inner, reach, tile), out_shape...]
    concatenate x2 -> x0, other arithmetic: 1.97 us -> none  [rotate(): jnp.concatenate([lower_half * cos_b - upper_half * sin_b, upper_half * co...]
    unnamed x10 -> x2, local copies, waits for them, and re-layouts: 1.74 us -> 0.01 us
    cos x1 -> x0, other arithmetic: 1.7 us -> none  [rotary_tables(): return (jnp.cos(angle), jnp.sin(angle))]
    another operation x2 -> x0, other arithmetic: 1.6 us -> none  [the longest x1 0.81 us: on_device(): pair = jnp.stack([rot_k, values], axis=0)]
    unnamed x1 -> x0, other arithmetic: 1.47 us -> none
where the time goes in v3:
time: 136 us; the launch traced here: 135 us
  Pallas kernels  132 us (97%)
  other arithmetic  3.41 us (3%)
    pallas_call x1, Pallas kernels, on_device(): pl.pallas_call(functools.partial(fused, n, inner, reach, tile), out_shape...  132 us
    convert_element_type x1, other arithmetic, on_device(): (gathered.astype(jnp.float32) + residual.astype(jnp.float32)).astype(jnp....  3.41 us

profile of v3, /device:TPU:0, one launch (start us, length us, event | category | flops | bytes accessed | tf_op | source)
XLA Modules:
  0.0 135.4 jit_solution(17967227484013247175)
XLA Ops:
  0.0 0.0 copy-start
  0.0 131.9 %shard_map.82 = bf16[128,8192]{1,0:T(8,128)(2,1)} custom-call(bf16[512,1024]{1,0:T(8,128)(2,1)} %q_ref.1, bf16[512,128]{1,0:T(8,128)(2,1)} %k_ref.1, bf16[512,128]{1,0:T(8,128)(2,1)} %v_ref.1, s32[3,512]{1,0:T(4,128)} %place_ref.1, s32[1,4096]{1,0:T(1,128)} %bitcast.1, f32[64,1]{1,0:T(8,128)} %constant.2.clone.freq_ref, bf16[1024,1024]{1,0:T(8,128)(2,1)} %w_ref.1), custom_call_target="tpu_custom_call" | custom-call | tf_op jit(solution)/shard_map/pallas_call | solution.py:549
  132.0 0.0 copy-done
  132.0 3.4 %add_convert_fusion = bf16[128,8192]{1,0:T(8,128)(2,1)} fusion(bf16[128,8192]{1,0:T(8,128)(2,1)S(1)} %copy-done, bf16[128,8192]{1,0:T(8,128)(2,1)} %shard_map.82), kind=kLoop, calls=%fused_computation | loop fusion | flops 4194304 | bytes 6291456 | tf_op jit(solution)/shard_map/convert_element_type | solution.py:579
Async XLA Ops:
  0.0 132.0 %copy-start = (bf16[128,8192]{1,0:T(8,128)(2,1)S(1)}, bf16[128,8192]{1,0:T(8,128)(2,1)}, u32[]{:S(2)}) copy-start(bf16[128,8192]{1,0:T(8,128)(2,1)} %param.14) | copy-start | bytes 6291460

commit v4 on v3

--- a/solution.py
+++ b/solution.py
@@ -18,14 +18,15 @@
 
 def half_frequencies():
     index = np.arange(HD // 2, dtype=np.float64)
-    return np.power(theta_base, -2.0 * index / HD).astype(np.float32)[:, None]
+    values = np.power(theta_base, -2.0 * index / HD).astype(np.float32)
+    return np.broadcast_to(values[:, None], (HD // 2, HD)).copy()
 
 
 def fused(
     n, inner, reach, tile,
-    q_ref, k_ref, v_ref, place_ref, segment_ref, freq_ref, w_ref, out_ref,
-    cosine, sine, my_segment, segments, kvbuf, wbuf, att, abuf, bias, pbuf, xrecv, obuf,
-    kv_s, kv_r, w_r, wu_s, wd_s, wm_s, a_s, a_r, ha_s, hf_s, ha_r, x_s, x_r, o_s, o_r,
+    k_hbm, v_hbm, place_hbm, segment_hbm, freq_hbm, q_hbm, w_ref, out_ref,
+    k_ref, v_ref, place_ref, segment_ref, freq_ref, q_ref, cosine, sine, my_segment, segments, kvbuf, wbuf, att, abuf, bias, pbuf, xrecv, obuf,
+    in_s, kv_s, kv_r, w_r, wu_s, wd_s, wm_s, a_s, a_r, ha_s, hf_s, ha_r, x_s, x_r, o_s, o_r,
 ):
     outer = n // inner
     tok = q_ref.shape[0]
@@ -64,6 +65,15 @@
             w_ref.at[:, j * cut:(j + 1) * cut], wbuf.at[co, h, j], w_r.at[co, h, j]
         )
 
+    moves = [
+        pltpu.make_async_copy(src, dst, in_s.at[k]) for k, (src, dst) in enumerate([
+            (place_hbm, place_ref), (freq_hbm, freq_ref), (k_hbm, k_ref), (v_hbm, v_ref),
+            (segment_hbm, segment_ref), (q_hbm, q_ref),
+        ])
+    ]
+    q_copy = moves[-1]
+    for move in moves:
+        move.start()
     for j in range(pieces):
         own_piece(j).start()
 
@@ -91,6 +101,109 @@
     def turned(vectors, at):
         wide = vectors.astype(jnp.float32)
         return (wide * cosine[at, :] + pltpu.roll(wide, HD // 2, 1) * sine[at, :]).astype(jnp.bfloat16)
+
+    pl.semaphore_wait(barrier, 2 * inner + 2 * inner * beside)
+    for move in moves[:-1]:
+        move.wait()
+
+    half = tok // 2
+    kv_parts = 4
+
+    def kv_slot(d, part):
+        start = pl.multiple_of((reach - d) * tok + part % 2 * half, half)
+        return kvbuf.at[part // 2, pl.ds(start, half), :]
+
+    def kv_sends(s, part, action):
+        src = kv_slot(s * inner, part)
+        if s == 0 and part // 2 == 1:
+            src = v_ref.at[pl.ds(part % 2 * half, half), :]
+
+        def one(k, slot, device):
+            action(remote(src, kv_slot(slot, part), kv_s.at[s, k], kv_r.at[slot - 1, part], device))
+
+        if not chained:
+            for d in range(1, reach + 1):
+                @pl.when(c + d < n)
+                def _():
+                    one(d, d, {"ctx": c + d, "tp": t})
+            return
+
+        @pl.when(co >= s)
+        def _():
+            if (s + 1) * inner <= reach:
+                @pl.when(co < last)
+                def _():
+                    one(0, (s + 1) * inner, {"ctx": c + inner, "tp": t})
+            for k in range(1, inner):
+                near = (ci + k) % inner
+                away = s * inner + near - ci
+
+                @pl.when((away >= 1) & (away <= reach))
+                def _():
+                    one(k, away, {"ctx": co * inner + near, "tp": t})
+
+    stages = reach // inner + 1 if chained else 1
+    for part in range(2, kv_parts):
+        kv_sends(0, part, lambda copy: copy.start())
+
+    early = (pieces + 1) // 2
+    shared = pieces * 5 // 8
+
+    def w_up(slot, j):
+        device = {"ctx": c + inner, "tp": t}
+        return remote(wbuf.at[slot, h, j], wbuf.at[slot, h, j], wu_s.at[slot], w_r.at[slot, h, j], device)
+
+    def w_down(slot, j):
+        device = {"ctx": c - inner, "tp": t}
+        return remote(wbuf.at[slot, h, j], wbuf.at[slot, h, j], wd_s.at[slot], w_r.at[slot, h, j], device)
+
+    def w_mate(slot, j):
+        return remote(wbuf.at[slot, h, j], wbuf.at[slot, h, j], wm_s.at[slot], w_r.at[slot, h, j], mate)
+
+    def near_end(away, j):
+        return (away <= 1) | ((away == 2) & (j < shared))
+
+    def goes_up(slot, j):
+        return (slot <= co) & (co < last) & ((co + 1 < last) | near_end(co + 1 - slot, j))
+
+    def goes_down(slot, j):
+        return (slot >= co) & (co > 0) & ((co > 1) | near_end(slot - co + 1, j))
+
+    def has(slot, j):
+        return jnp.logical_not(is_end) | (near_end(slot - co, j) & near_end(co - slot, j))
+
+    def lends(slot, j):
+        away = jnp.where(slot < helped, helped - slot, slot - helped)
+        return helps & jnp.logical_not(near_end(away, j))
+
+    def pass_up(slot, j):
+        @pl.when(goes_up(slot, j))
+        def _():
+            w_up(slot, j).start()
+
+    def pass_down(slot, j):
+        @pl.when(goes_down(slot, j))
+        def _():
+            w_down(slot, j).start()
+
+    def own_up():
+        for j in range(pieces):
+            if j < early:
+                pass_up(co, j)
+            else:
+                @pl.when(jnp.logical_not(is_end))
+                def _():
+                    pass_up(co, j)
+
+    for j in range(pieces):
+        own_piece(j).wait()
+        if j < early:
+            pass_down(co, j)
+        else:
+            @pl.when(jnp.logical_not(is_end))
+            def _():
+                pass_down(co, j)
+        w_mate(co, j).start()
 
     everything = pl.ds(0, tok)
     frequency = lax.broadcasted_iota(jnp.int32, (HD // 2, tok), 0)
@@ -100,112 +213,14 @@
     chosen = jnp.where(
         frequency < first_end, place[0:1], jnp.where(frequency < second_end, place[1:2], place[2:3])
     )
-    angle = chosen * freq_ref[...]
+    angle = chosen * freq_ref[:, 0:1]
     cos_part, sin_part = jnp.cos(angle), jnp.sin(angle)
     cosine[...] = jnp.concatenate([cos_part, cos_part], axis=0).T
     sine[...] = jnp.concatenate([-sin_part, sin_part], axis=0).T
     kvbuf[0, reach * tok:, :] = turned(k_ref[...], everything)
     kvbuf[1, reach * tok:, :] = v_ref[...]
-    pl.semaphore_wait(barrier, 2 * inner + 2 * inner * beside)
-
-    half = tok // 2
-    kv_parts = 4
-
-    def kv_slot(d, part):
-        start = pl.multiple_of((reach - d) * tok + part % 2 * half, half)
-        return kvbuf.at[part // 2, pl.ds(start, half), :]
-
-    def kv_sends(s, part, action):
-        src = kv_slot(s * inner, part)
-        if s == 0 and part // 2 == 1:
-            src = v_ref.at[pl.ds(part % 2 * half, half), :]
-
-        def one(k, slot, device):
-            action(remote(src, kv_slot(slot, part), kv_s.at[s, k, part], kv_r.at[slot - 1, part], device))
-
-        if not chained:
-            for d in range(1, reach + 1):
-                @pl.when(c + d < n)
-                def _():
-                    one(d, d, {"ctx": c + d, "tp": t})
-            return
-
-        @pl.when(co >= s)
-        def _():
-            if (s + 1) * inner <= reach:
-                @pl.when(co < last)
-                def _():
-                    one(0, (s + 1) * inner, {"ctx": c + inner, "tp": t})
-            for k in range(1, inner):
-                near = (ci + k) % inner
-                away = s * inner + near - ci
-
-                @pl.when((away >= 1) & (away <= reach))
-                def _():
-                    one(k, away, {"ctx": co * inner + near, "tp": t})
-
-    stages = reach // inner + 1 if chained else 1
-    for part in range(kv_parts):
+    for part in range(2):
         kv_sends(0, part, lambda copy: copy.start())
-
-    early = (pieces + 1) // 2
-    shared = pieces // 2
-
-    def w_up(slot, j):
-        device = {"ctx": c + inner, "tp": t}
-        return remote(wbuf.at[slot, h, j], wbuf.at[slot, h, j], wu_s.at[slot, j], w_r.at[slot, h, j], device)
-
-    def w_down(slot, j):
-        device = {"ctx": c - inner, "tp": t}
-        return remote(wbuf.at[slot, h, j], wbuf.at[slot, h, j], wd_s.at[slot, j], w_r.at[slot, h, j], device)
-
-    def w_mate(slot, j):
-        return remote(wbuf.at[slot, h, j], wbuf.at[slot, h, j], wm_s.at[slot, j], w_r.at[slot, h, j], mate)
-
-    def near_end(away, j):
-        return (away <= 1) | ((away == 2) & (j < shared))
-
-    def goes_up(slot, j):
-        return (slot <= co) & (co < last) & ((co + 1 < last) | near_end(co + 1 - slot, j))
-
-    def goes_down(slot, j):
-        return (slot >= co) & (co > 0) & ((co > 1) | near_end(slot - co + 1, j))
-
-    def has(slot, j):
-        return jnp.logical_not(is_end) | (near_end(slot - co, j) & near_end(co - slot, j))
-
-    def lends(slot, j):
-        away = jnp.where(slot < helped, helped - slot, slot - helped)
-        return helps & jnp.logical_not(near_end(away, j))
-
-    def pass_up(slot, j):
-        @pl.when(goes_up(slot, j))
-        def _():
-            w_up(slot, j).start()
-
-    def pass_down(slot, j):
-        @pl.when(goes_down(slot, j))
-        def _():
-            w_down(slot, j).start()
-
-    def own_up():
-        for j in range(pieces):
-            if j < early:
-                pass_up(co, j)
-            else:
-                @pl.when(jnp.logical_not(is_end))
-                def _():
-                    pass_up(co, j)
-
-    for j in range(pieces):
-        own_piece(j).wait()
-        if j < early:
-            pass_down(co, j)
-        else:
-            @pl.when(jnp.logical_not(is_end))
-            def _():
-                pass_down(co, j)
-        w_mate(co, j).start()
 
     @pl.when(co == 0)
     def _():
@@ -236,7 +251,7 @@
     lax.fori_loop(0, tiles, fill_bias, 0)
 
     for s in range(1, stages):
-        for part in range(kv_parts):
+        for part in (2, 3, 0, 1):
             @pl.when(co >= s)
             def _():
                 landed(kv_slot(s * inner, part), kv_r.at[s * inner - 1, part])
@@ -259,6 +274,7 @@
                 for part in range(kv_parts):
                     landed(kv_slot(d, part), kv_r.at[d - 1, part])
 
+    q_copy.wait()
     factor = math.log2(math.e) / math.sqrt(HD)
 
     def rows_of(side, at):
@@ -282,7 +298,7 @@
                         @pl.when(is_end)
                         def _():
                             action(remote(
-                                src, abuf.at[1, h, rows_of(side, ci), lanes], ha_s.at[gg],
+                                src, abuf.at[1, h, rows_of(side, ci), lanes], ha_s,
                                 ha_r.at[ci, h, side], {"ctx": helper * inner + ci, "tp": 2 * x + g},
                             ))
 
@@ -360,7 +376,7 @@
     def x_copy(who, slot, j):
         return remote(
             pbuf.at[who, slot, j, other_x], xrecv.at[who, slot, j],
-            x_s.at[who, slot, j], x_r.at[who, slot, j], across,
+            x_s.at[who, slot], x_r.at[who, slot, j], across,
         )
 
     def out_slot(slot, j, at):
@@ -372,7 +388,7 @@
         device = {"ctx": node * inner + near, "tp": t}
         return remote(
             obuf.at[who, slot, j, near], out_slot(slot, j, ci),
-            o_s.at[who, slot, j, k], o_r.at[slot, j, ci], device,
+            o_s.at[who, slot], o_r.at[slot, ci], device,
         )
 
     def job(who, slot, j):
@@ -405,10 +421,14 @@
                 for side in range(2):
                     here = abuf.at[1, g, rows_of(side, ci), :]
                     action(remote(
-                        here, here, hf_s.at[k, g, side], ha_r.at[ci, g, side],
+                        here, here, hf_s, ha_r.at[ci, g, side],
                         {"ctx": co * inner + near, "tp": t},
                     ))
 
+    lag = min(5, pieces + 2)
+    ahead = min(2, early)
+    forward_at = max(1, min(5, pieces - 1))
+
     def step(i, _):
         d, j = i // pieces, i % pieces
 
@@ -416,7 +436,7 @@
         def _():
             each_side(d, j, lambda slot: arrive(slot, j))
 
-        @pl.when(helps & (i == 1))
+        @pl.when(helps & (i == forward_at))
         def _():
             for g in range(2):
                 for side in range(2):
@@ -468,17 +488,35 @@
         def _():
             finish(1, beyond, j)
 
-        @pl.when((d == 1) & (j + early < pieces))
-        def _():
-            each_side(1, j, lambda slot: arrive(slot, j + early))
+        @pl.when((d == 1) & (j + ahead >= early) & (j + ahead < pieces))
+        def _():
+            each_side(1, j, lambda slot: arrive(slot, j + ahead))
         return 0
 
-    lag = min(5, pieces + 2)
     lax.fori_loop(0, outer * pieces + lag, step, 0)
 
-    for s in range(stages):
-        for part in range(kv_parts):
-            kv_sends(s, part, lambda copy: copy.wait_send())
+    def kv_sent(s, k):
+        landed(kvbuf.at[:, 0:tok, :], kv_s.at[s, k])
+
+    if chained:
+        for s in range(stages):
+            @pl.when(co >= s)
+            def _():
+                if (s + 1) * inner <= reach:
+                    @pl.when(co < last)
+                    def _():
+                        kv_sent(s, 0)
+                for k in range(1, inner):
+                    away = s * inner + (ci + k) % inner - ci
+
+                    @pl.when((away >= 1) & (away <= reach))
+                    def _():
+                        kv_sent(s, k)
+    else:
+        for d in range(1, reach + 1):
+            @pl.when(c + d < n)
+            def _():
+                kv_sent(0, d)
     for k in range(inner):
         for gg in range(2):
             if k + gg > 0:
@@ -486,49 +524,79 @@
 
     @pl.when(is_end)
     def _():
-        for gg in range(2):
-            landed(abuf.at[0, 0, 0:2 * quarter, :], ha_s.at[gg])
+        landed(abuf.at[0, :, 0:2 * quarter, :], ha_s)
 
     @pl.when(helps)
     def _():
-        forwards(lambda copy: copy.wait_send())
-
-    def drain(i, _):
-        slot, j = i // pieces, i % pieces
-
-        @pl.when(has(slot, j))
-        def _():
-            w_mate(slot, j).wait_send()
-
-            @pl.when(goes_up(slot, j))
-            def _():
-                w_up(slot, j).wait_send()
-
-            @pl.when(goes_down(slot, j))
-            def _():
-                w_down(slot, j).wait_send()
-
-            x_copy(0, slot, j).wait_send()
-            for k in range(1, inner):
-                o_copy(0, slot, j, k).wait_send()
-
-        @pl.when(lends(slot, j))
-        def _():
-            x_copy(1, slot, j).wait_send()
-            for k in range(inner):
-                o_copy(1, slot, j, k).wait_send()
-
-        for k in range(inner):
+        landed(abuf.at[1, :, 0:2 * quarter * (inner - 1), :], hf_s)
+
+    def drain(slot, _):
+        def parted(action):
+            whole_unit = has(slot, pieces - 1)
+
+            @pl.when(whole_unit)
+            def _():
+                action(pieces)
+
+            if shared:
+                @pl.when(has(slot, 0) & jnp.logical_not(whole_unit))
+                def _():
+                    action(shared)
+
+        def sent(count):
+            landed(wbuf.at[slot, h, 0:count], wm_s.at[slot])
+            landed(xrecv.at[0, slot, 0:count], x_s.at[0, slot])
+            landed(obuf.at[0, slot, 0:count, 0:inner - 1], o_s.at[0, slot])
+
+        parted(sent)
+
+        def moved(goes, sem):
+            whole_unit = goes(slot, pieces - 1)
+
+            @pl.when(whole_unit)
+            def _():
+                landed(wbuf.at[slot, h], sem)
+
+            if shared:
+                @pl.when(goes(slot, 0) & jnp.logical_not(whole_unit))
+                def _():
+                    landed(wbuf.at[slot, h, 0:shared], sem)
+
+        moved(goes_up, wu_s.at[slot])
+        moved(goes_down, wd_s.at[slot])
+
+        def lent(start):
+            landed(xrecv.at[1, slot, start:pieces], x_s.at[1, slot])
+            landed(obuf.at[1, slot, start:pieces], o_s.at[1, slot])
+
+        @pl.when(lends(slot, 0))
+        def _():
+            lent(0)
+
+        if shared:
+            @pl.when(lends(slot, pieces - 1) & jnp.logical_not(lends(slot, 0)))
+            def _():
+                lent(shared)
+
+        def unit(at, start):
+            first = pl.multiple_of((slot * inner + at) * cols + start * cut, 128)
+            return out_ref.at[:, pl.ds(first, cols - start * cut)]
+
+        @pl.when(jnp.logical_not(has(slot, 0)))
+        def _():
+            landed(unit(ci, 0), o_r.at[slot, ci])
+
+        if shared:
+            @pl.when(has(slot, 0) & jnp.logical_not(has(slot, pieces - 1)))
+            def _():
+                landed(unit(ci, shared), o_r.at[slot, ci])
+
+        for k in range(1, inner):
             near = (ci + k) % inner
-            if k == 0:
-                @pl.when(jnp.logical_not(has(slot, j)))
-                def _():
-                    landed(out_slot(slot, j, near), o_r.at[slot, j, near])
-            else:
-                landed(out_slot(slot, j, near), o_r.at[slot, j, near])
+            landed(unit(near, 0), o_r.at[slot, near])
         return 0
 
-    lax.fori_loop(0, outer * pieces, drain, 0)
+    lax.fori_loop(0, outer, drain, 0)
 
 
 def on_device(queries, keys, values, positions, segment_ids, out_weight, residual):
@@ -549,9 +617,15 @@
     gathered = pl.pallas_call(
         functools.partial(fused, n, inner, reach, tile),
         out_shape=jax.ShapeDtypeStruct((quarter, n * cols), bf16),
-        in_specs=[vmem] * 6 + [pl.BlockSpec(memory_space=pl.ANY)],
+        in_specs=[pl.BlockSpec(memory_space=pltpu.HBM)] * 7,
         out_specs=vmem,
         scratch_shapes=[
+            pltpu.VMEM((tok, HD), bf16),
+            pltpu.VMEM((tok, HD), bf16),
+            pltpu.VMEM(positions.shape, jnp.int32),
+            pltpu.VMEM((1, n * tok), jnp.int32),
+            pltpu.VMEM((HD // 2, HD), jnp.float32),
+            pltpu.VMEM((tok, depth), bf16),
             pltpu.VMEM((tok, HD), jnp.float32),
             pltpu.VMEM((tok, HD), jnp.float32),
             pltpu.VMEM((tok, HD), jnp.float32),
@@ -564,18 +638,18 @@
             pltpu.VMEM((2, outer, pieces, 2, block, cut), bf16),
             pltpu.VMEM((2, outer, pieces, block, cut), bf16),
             pltpu.VMEM((2, outer, pieces, inner, quarter, cut), bf16),
-            dma((reach + 1, max(inner, reach + 1), 4)), dma((reach, 4)),
-            dma((outer, 2, pieces)),
-            dma((outer, pieces)), dma((outer, pieces)), dma((outer, pieces)),
+            dma((6,)),
+            dma((reach // inner + 1, inner) if reach % inner == 0 else (1, reach + 1)), dma((reach, 4)),
+            dma((outer, 2, pieces)), dma((outer,)), dma((outer,)), dma((outer,)),
             dma((inner, 2)), dma((inner, 2, 2)),
-            dma((2,)), dma((inner, 2, 2)), dma((inner, 2, 2)),
-            dma((2, outer, pieces)), dma((2, outer, pieces)),
-            dma((2, outer, pieces, inner)), dma((outer, pieces, inner)),
+            dma, dma, dma((inner, 2, 2)),
+            dma((2, outer)), dma((2, outer, pieces)),
+            dma((2, outer)), dma((outer, inner)),
         ],
         compiler_params=pltpu.CompilerParams(
             collective_id=0, has_side_effects=True, vmem_limit_bytes=60 * 1024 * 1024
         ),
-    )(queries, keys, values, positions, segment_ids[None, :], half_frequencies(), out_weight)
+    )(keys, values, positions, segment_ids[None, :], half_frequencies(), queries, out_weight)
     return (gathered.astype(jnp.float32) + residual.astype(jnp.float32)).astype(jnp.bfloat16)
 
 

time: 136 us -> 126 us (0.926)
  Pallas kernels: 132 us -> 122 us
    pallas_call x1, Pallas kernels: 132 us -> 122 us  [on_device(): pl.pallas_call(functools.partial(fused, n, inner, reach, tile), out_shape...]
where the time goes in v4:
time: 126 us; the launch traced here: 125 us
  Pallas kernels  122 us (97%)
  other arithmetic  3.41 us (3%)
    pallas_call x1, Pallas kernels, on_device(): pl.pallas_call(functools.partial(fused, n, inner, reach, tile), out_shape...  122 us
    convert_element_type x1, other arithmetic, on_device(): (gathered.astype(jnp.float32) + residual.astype(jnp.float32)).astype(jnp....  3.41 us

profile of v4, /device:TPU:0, one launch (start us, length us, event | category | flops | bytes accessed | tf_op | source)
XLA Modules:
  0.0 125.0 jit_solution(12846932705418869545)
XLA Ops:
  0.0 0.0 copy-start
  0.0 121.6 %shard_map.82 = bf16[128,8192]{1,0:T(8,128)(2,1)} custom-call(bf16[512,128]{1,0:T(8,128)(2,1)} %k_hbm.1, bf16[512,128]{1,0:T(8,128)(2,1)} %v_hbm.1, s32[3,512]{1,0:T(4,128)} %place_hbm.1, s32[1,4096]{1,0:T(1,128)} %bitcast.1, f32[64,128]{1,0:T(8,128)} %constant.2.clone.freq_hbm, bf16[512,1024]{1,0:T(8,128)(2,1)} %q_hbm.1, bf16[1024,1024]{1,0:T(8,128)(2,1)} %w_ref.1), custom_call_target="tpu_custom_call" | custom-call | tf_op jit(solution)/shard_map/pallas_call | solution.py:617
  121.6 0.0 copy-done
  121.6 3.4 %add_convert_fusion = bf16[128,8192]{1,0:T(8,128)(2,1)} fusion(bf16[128,8192]{1,0:T(8,128)(2,1)S(1)} %copy-done, bf16[128,8192]{1,0:T(8,128)(2,1)} %shard_map.82), kind=kLoop, calls=%fused_computation | loop fusion | flops 4194304 | bytes 6291456 | tf_op jit(solution)/shard_map/convert_element_type | solution.py:653
Async XLA Ops:
  0.0 121.6 %copy-start = (bf16[128,8192]{1,0:T(8,128)(2,1)S(1)}, bf16[128,8192]{1,0:T(8,128)(2,1)}, u32[]{:S(2)}) copy-start(bf16[128,8192]{1,0:T(8,128)(2,1)} %param.14) | copy-start | bytes 6291460

commit v5 on v4

--- a/solution.py
+++ b/solution.py
@@ -24,9 +24,9 @@
 
 def fused(
     n, inner, reach, tile,
-    k_hbm, v_hbm, place_hbm, segment_hbm, freq_hbm, q_hbm, w_ref, out_ref,
-    k_ref, v_ref, place_ref, segment_ref, freq_ref, q_ref, cosine, sine, my_segment, segments, kvbuf, wbuf, att, abuf, bias, pbuf, xrecv, obuf,
-    in_s, kv_s, kv_r, w_r, wu_s, wd_s, wm_s, a_s, a_r, ha_s, hf_s, ha_r, x_s, x_r, o_s, o_r,
+    k_hbm, v_hbm, place_hbm, segment_hbm, freq_hbm, q_hbm, residual_hbm, w_ref, result_hbm,
+    k_ref, v_ref, place_ref, segment_ref, freq_ref, q_ref, residual_ref, out_ref, cosine, sine, my_segment, segments, kvbuf, wbuf, att, abuf, bias, pbuf, xrecv, obuf,
+    in_s, out_s, kv_s, kv_r, w_r, wu_s, wd_s, wm_s, a_s, a_r, ha_s, hf_s, ha_r, x_s, x_r, o_s, o_r,
 ):
     outer = n // inner
     tok = q_ref.shape[0]
@@ -68,11 +68,11 @@
     moves = [
         pltpu.make_async_copy(src, dst, in_s.at[k]) for k, (src, dst) in enumerate([
             (place_hbm, place_ref), (freq_hbm, freq_ref), (k_hbm, k_ref), (v_hbm, v_ref),
-            (segment_hbm, segment_ref), (q_hbm, q_ref),
+            (segment_hbm, segment_ref), (q_hbm, q_ref), (residual_hbm, residual_ref),
         ])
     ]
-    q_copy = moves[-1]
-    for move in moves:
+    q_copy, residual_copy = moves[-2:]
+    for move in moves[:-1]:
         move.start()
     for j in range(pieces):
         own_piece(j).start()
@@ -103,7 +103,8 @@
         return (wide * cosine[at, :] + pltpu.roll(wide, HD // 2, 1) * sine[at, :]).astype(jnp.bfloat16)
 
     pl.semaphore_wait(barrier, 2 * inner + 2 * inner * beside)
-    for move in moves[:-1]:
+    residual_copy.start()
+    for move in moves[:-2]:
         move.wait()
 
     half = tok // 2
@@ -275,6 +276,7 @@
                     landed(kv_slot(d, part), kv_r.at[d - 1, part])
 
     q_copy.wait()
+    residual_copy.wait()
     factor = math.log2(math.e) / math.sqrt(HD)
 
     def rows_of(side, at):
@@ -391,6 +393,9 @@
             o_s.at[who, slot], o_r.at[slot, ci], device,
         )
 
+    def plus_residual(summed, at):
+        return (summed.astype(jnp.float32) + residual_ref[:, at].astype(jnp.float32)).astype(jnp.bfloat16)
+
     def job(who, slot, j):
         for side in range(2):
             at = slice(side * block, (side + 1) * block)
@@ -410,7 +415,8 @@
         for k in range(1 - who, inner):
             o_copy(who, slot, j, k).start()
         if not who:
-            out_ref[:, pl.ds(pl.multiple_of((slot * inner + ci) * cols + j * cut, 128), cut)] = obuf[who, slot, j, ci]
+            at = pl.ds(pl.multiple_of((slot * inner + ci) * cols + j * cut, 128), cut)
+            out_ref[:, at] = plus_residual(obuf[who, slot, j, ci], at)
 
     beyond = 2 * co - helped
 
@@ -426,6 +432,12 @@
                     ))
 
     lag = min(5, pieces + 2)
+    late_lag = jnp.where(2 * co >= outer, 1, 2)
+
+    def done_by(i):
+        behind = jnp.where(i < 2 * pieces, lag, late_lag)
+        return jnp.clip(i - behind + 1, 0, outer * pieces)
+
     ahead = min(2, early)
     forward_at = max(1, min(5, pieces - 1))
 
@@ -470,11 +482,9 @@
         def _():
             each_side(d, j, begins)
 
-        before = i - lag
-        then = before % pieces
-
-        @pl.when(before >= 0)
-        def _():
+        def end_of(before, _):
+            then = before % pieces
+
             def ends(slot):
                 @pl.when(lends(slot, then) & (before >= 2 * pieces))
                 def _():
@@ -483,6 +493,9 @@
                 finish(0, slot, then)
 
             each_side(before // pieces, then, ends)
+            return 0
+
+        lax.fori_loop(done_by(i - 1), done_by(i), end_of, 0)
 
         @pl.when(helps & (d == 2) & (j >= shared))
         def _():
@@ -493,7 +506,7 @@
             each_side(1, j, lambda slot: arrive(slot, j + ahead))
         return 0
 
-    lax.fori_loop(0, outer * pieces + lag, step, 0)
+    lax.fori_loop(0, outer * pieces + 2, step, 0)
 
     def kv_sent(s, k):
         landed(kvbuf.at[:, 0:tok, :], kv_s.at[s, k])
@@ -578,25 +591,59 @@
             def _():
                 lent(shared)
 
-        def unit(at, start):
-            first = pl.multiple_of((slot * inner + at) * cols + start * cut, 128)
-            return out_ref.at[:, pl.ds(first, cols - start * cut)]
-
+        return 0
+
+    def place_of(slot, at):
+        return pl.multiple_of((slot * inner + at) * cols, 128)
+
+    def store(slot, at):
+        where = pl.ds(place_of(slot, at), cols)
+        return pltpu.make_async_copy(out_ref.at[:, where], result_hbm.at[:, where], out_s.at[slot, at])
+
+    def settle(slot, at, start):
+        first = pl.multiple_of(place_of(slot, at) + start * cut, 128)
+        landed(out_ref.at[:, pl.ds(first, cols - start * cut)], o_r.at[slot, at])
+        for j in range(start, pieces):
+            where = pl.ds(pl.multiple_of(place_of(slot, at) + j * cut, 128), cut)
+            out_ref[:, where] = plus_residual(out_ref[:, where], where)
+
+    def collect(slot):
         @pl.when(jnp.logical_not(has(slot, 0)))
         def _():
-            landed(unit(ci, 0), o_r.at[slot, ci])
+            settle(slot, ci, 0)
 
         if shared:
             @pl.when(has(slot, 0) & jnp.logical_not(has(slot, pieces - 1)))
             def _():
-                landed(unit(ci, shared), o_r.at[slot, ci])
-
+                settle(slot, ci, shared)
+
+        store(slot, ci).start()
         for k in range(1, inner):
             near = (ci + k) % inner
-            landed(unit(near, 0), o_r.at[slot, near])
+            settle(slot, near, 0)
+            store(slot, near).start()
+
+    def collect_at(distance, _):
+        def one_side(side, _):
+            slot = co + distance * (2 * side - 1)
+
+            @pl.when((slot >= 0) & (slot < outer) & ((distance > 0) | (side == 1)))
+            def _():
+                collect(slot)
+            return 0
+
+        lax.fori_loop(0, 2, one_side, 0)
         return 0
 
+    lax.fori_loop(0, outer, collect_at, 0)
     lax.fori_loop(0, outer, drain, 0)
+
+    def stored(slot, _):
+        for at in range(inner):
+            store(slot, at).wait()
+        return 0
+
+    lax.fori_loop(0, outer, stored, 0)
 
 
 def on_device(queries, keys, values, positions, segment_ids, out_weight, residual):
@@ -613,12 +660,11 @@
     block = inner * quarter
     bf16 = jnp.bfloat16
     dma = pltpu.SemaphoreType.DMA
-    vmem = pl.BlockSpec(memory_space=pltpu.VMEM)
-    gathered = pl.pallas_call(
+    return pl.pallas_call(
         functools.partial(fused, n, inner, reach, tile),
         out_shape=jax.ShapeDtypeStruct((quarter, n * cols), bf16),
-        in_specs=[pl.BlockSpec(memory_space=pltpu.HBM)] * 7,
-        out_specs=vmem,
+        in_specs=[pl.BlockSpec(memory_space=pltpu.HBM)] * 8,
+        out_specs=pl.BlockSpec(memory_space=pltpu.HBM),
         scratch_shapes=[
             pltpu.VMEM((tok, HD), bf16),
             pltpu.VMEM((tok, HD), bf16),
@@ -626,6 +672,8 @@
             pltpu.VMEM((1, n * tok), jnp.int32),
             pltpu.VMEM((HD // 2, HD), jnp.float32),
             pltpu.VMEM((tok, depth), bf16),
+            pltpu.VMEM((quarter, n * cols), bf16),
+            pltpu.VMEM((quarter, n * cols), bf16),
             pltpu.VMEM((tok, HD), jnp.float32),
             pltpu.VMEM((tok, HD), jnp.float32),
             pltpu.VMEM((tok, HD), jnp.float32),
@@ -638,7 +686,7 @@
             pltpu.VMEM((2, outer, pieces, 2, block, cut), bf16),
             pltpu.VMEM((2, outer, pieces, block, cut), bf16),
             pltpu.VMEM((2, outer, pieces, inner, quarter, cut), bf16),
-            dma((6,)),
+            dma((7,)), dma((outer, inner)),
             dma((reach // inner + 1, inner) if reach % inner == 0 else (1, reach + 1)), dma((reach, 4)),
             dma((outer, 2, pieces)), dma((outer,)), dma((outer,)), dma((outer,)),
             dma((inner, 2)), dma((inner, 2, 2)),
@@ -649,8 +697,7 @@
         compiler_params=pltpu.CompilerParams(
             collective_id=0, has_side_effects=True, vmem_limit_bytes=60 * 1024 * 1024
         ),
-    )(keys, values, positions, segment_ids[None, :], half_frequencies(), queries, out_weight)
-    return (gathered.astype(jnp.float32) + residual.astype(jnp.float32)).astype(jnp.bfloat16)
+    )(keys, values, positions, segment_ids[None, :], half_frequencies(), queries, residual, out_weight)
 
 
 def solution(mesh):

time: 126 us -> 124 us (0.984)
  other arithmetic: 3.41 us -> 0 us
  local copies, waits for them, and re-layouts: 0.01 us -> 3.1 us
  Pallas kernels: 122 us -> 120 us
    convert_element_type x1 -> x0, other arithmetic: 3.41 us -> none  [on_device(): (gathered.astype(jnp.float32) + residual.astype(jnp.float32)).astype(jnp....]
    unnamed x2 -> x1, local copies, waits for them, and re-layouts: 0.01 us -> 3.1 us
    pallas_call x1, Pallas kernels: 122 us -> 120 us  [on_device(): pl.pallas_call(functools.partial(fused, n, inner, reach, tile), out_shape...]
where the time goes in v5:
time: 124 us; the launch traced here: 123 us
  Pallas kernels  120 us (97%)
  local copies, waits for them, and re-layouts  3.1 us (2%)
    pallas_call x1, Pallas kernels, on_device(): pl.pallas_call(functools.partial(fused, n, inner, reach, tile), out_shape...  120 us
    unnamed x1, local copies, waits for them, and re-layouts  3.1 us

profile of v5, /device:TPU:0, one launch (start us, length us, event | category | flops | bytes accessed | tf_op | source)
XLA Modules:
  0.0 123.5 jit_solution(15905148008401325913)
XLA Ops:
  0.0 120.3 %shard_map.82 = bf16[128,8192]{1,0:T(8,128)(2,1)} custom-call(bf16[512,128]{1,0:T(8,128)(2,1)} %k_hbm.1, bf16[512,128]{1,0:T(8,128)(2,1)} %v_hbm.1, s32[3,512]{1,0:T(4,128)} %place_hbm.1, s32[1,4096]{1,0:T(1,128)} %bitcast.1, f32[64,128]{1,0:T(8,128)} %constant.2.clone.freq_hbm, bf16[512,1024]{1,0:T(8,128)(2,1)} %q_hbm.1, bf16[128,8192]{1,0:T(8,128)(2,1)} %residual_hbm.1, ...), custom_call_target="tpu_custom_call" | custom-call | tf_op jit(solution)/shard_map/pallas_call | solution.py:663
  120.4 3.1 %copy.10 = bf16[128,8192]{1,0:T(8,128)(2,1)} copy(bf16[128,8192]{1,0:T(8,128)(2,1)} %shard_map.82) | data formatting | bytes 4194304

commit v6 on v5

--- a/solution.py
+++ b/solution.py
@@ -148,7 +148,7 @@
         kv_sends(0, part, lambda copy: copy.start())
 
     early = (pieces + 1) // 2
-    shared = pieces * 5 // 8
+    shared = pieces * 3 // 4
 
     def w_up(slot, j):
         device = {"ctx": c + inner, "tp": t}
@@ -432,14 +432,37 @@
                     ))
 
     lag = min(5, pieces + 2)
-    late_lag = jnp.where(2 * co >= outer, 1, 2)
 
     def done_by(i):
-        behind = jnp.where(i < 2 * pieces, lag, late_lag)
+        late = i - 2 * pieces
+        behind = jnp.where(
+            late < pieces // 4, lag, jnp.where(late < pieces // 2, 3, jnp.where(late < pieces - 1, 2, 1))
+        )
         return jnp.clip(i - behind + 1, 0, outer * pieces)
 
-    ahead = min(2, early)
     forward_at = max(1, min(5, pieces - 1))
+
+    first = jnp.where(helps, beyond, jnp.where(co > 0, co - 1, co + 1))
+
+    def items(i, action):
+        d, j = i // pieces, i % pieces
+        if pieces % 2:
+            each_side(d, j, lambda slot: action(slot, j))
+            return
+
+        @pl.when(d != 1)
+        def _():
+            each_side(d, j, lambda slot: action(slot, j))
+
+        slot = jnp.where(j < pieces // 2, first, 2 * co - first)
+
+        @pl.when((d == 1) & (slot >= 0) & (slot < outer))
+        def _():
+            def one(m, _):
+                action(slot, 2 * (j % (pieces // 2)) + m)
+                return 0
+
+            lax.fori_loop(0, 2, one, 0)
 
     def step(i, _):
         d, j = i // pieces, i % pieces
@@ -469,30 +492,28 @@
 
             lax.fori_loop(shared, pieces, lend, 0)
 
-        def begins(slot):
-            whole(slot, j)
-
-            @pl.when(lends(slot, j) & (d > 1))
-            def _():
-                job(1, slot, j)
-
-            job(0, slot, j)
+        def begins(slot, at):
+            whole(slot, at)
+
+            @pl.when(lends(slot, at) & (d > 1))
+            def _():
+                job(1, slot, at)
+
+            job(0, slot, at)
 
         @pl.when(d < outer)
         def _():
-            each_side(d, j, begins)
+            items(i, begins)
 
         def end_of(before, _):
-            then = before % pieces
-
-            def ends(slot):
-                @pl.when(lends(slot, then) & (before >= 2 * pieces))
-                def _():
-                    finish(1, slot, then)
-
-                finish(0, slot, then)
-
-            each_side(before // pieces, then, ends)
+            def ends(slot, at):
+                @pl.when(lends(slot, at) & (before >= 2 * pieces))
+                def _():
+                    finish(1, slot, at)
+
+                finish(0, slot, at)
+
+            items(before, ends)
             return 0
 
         lax.fori_loop(done_by(i - 1), done_by(i), end_of, 0)
@@ -501,9 +522,14 @@
         def _():
             finish(1, beyond, j)
 
-        @pl.when((d == 1) & (j + ahead >= early) & (j + ahead < pieces))
-        def _():
-            each_side(1, j, lambda slot: arrive(slot, j + ahead))
+        @pl.when((i + 1) // pieces == 1)
+        def _():
+            def later(slot, at):
+                @pl.when(at >= early)
+                def _():
+                    arrive(slot, at)
+
+            items(i + 1, later)
         return 0
 
     lax.fori_loop(0, outer * pieces + 2, step, 0)

time: 124 us -> 121 us (0.976)
  Pallas kernels: 120 us -> 117 us
    pallas_call x1, Pallas kernels: 120 us -> 117 us  [on_device(): pl.pallas_call(functools.partial(fused, n, inner, reach, tile), out_shape...]
where the time goes in v6:
time: 121 us; the launch traced here: 120 us
  Pallas kernels  117 us (97%)
  local copies, waits for them, and re-layouts  3.1 us (3%)
    pallas_call x1, Pallas kernels, on_device(): pl.pallas_call(functools.partial(fused, n, inner, reach, tile), out_shape...  117 us
    unnamed x1, local copies, waits for them, and re-layouts  3.1 us

profile of v6, /device:TPU:0, one launch (start us, length us, event | category | flops | bytes accessed | tf_op | source)
XLA Modules:
  0.0 120.4 jit_solution(3318903256720217327)
XLA Ops:
  0.0 117.3 %shard_map.82 = bf16[128,8192]{1,0:T(8,128)(2,1)} custom-call(bf16[512,128]{1,0:T(8,128)(2,1)} %k_hbm.1, bf16[512,128]{1,0:T(8,128)(2,1)} %v_hbm.1, s32[3,512]{1,0:T(4,128)} %place_hbm.1, s32[1,4096]{1,0:T(1,128)} %bitcast.1, f32[64,128]{1,0:T(8,128)} %constant.2.clone.freq_hbm, bf16[512,1024]{1,0:T(8,128)(2,1)} %q_hbm.1, bf16[128,8192]{1,0:T(8,128)(2,1)} %residual_hbm.1, ...), custom_call_target="tpu_custom_call" | custom-call | tf_op jit(solution)/shard_map/pallas_call | solution.py:689
  117.3 3.1 %copy.10 = bf16[128,8192]{1,0:T(8,128)(2,1)} copy(bf16[128,8192]{1,0:T(8,128)(2,1)} %shard_map.82) | data formatting | bytes 4194304

commit v7 on v6

--- a/solution.py
+++ b/solution.py
@@ -148,7 +148,7 @@
         kv_sends(0, part, lambda copy: copy.start())
 
     early = (pieces + 1) // 2
-    shared = pieces * 3 // 4
+    shared = pieces * 7 // 8
 
     def w_up(slot, j):
         device = {"ctx": c + inner, "tp": t}
@@ -397,13 +397,16 @@
         return (summed.astype(jnp.float32) + residual_ref[:, at].astype(jnp.float32)).astype(jnp.bfloat16)
 
     def job(who, slot, j):
-        for side in range(2):
-            at = slice(side * block, (side + 1) * block)
+        def one(side):
+            at = pl.ds(pl.multiple_of(side * block, block), block)
             pbuf[who, slot, j, side] = (
                 jnp.dot(abuf[who, 0, at, :], wbuf[slot, 0, j], preferred_element_type=jnp.float32)
                 + jnp.dot(abuf[who, 1, at, :], wbuf[slot, 1, j], preferred_element_type=jnp.float32)
             ).astype(jnp.bfloat16)
+
+        one(other_x)
         x_copy(who, slot, j).start()
+        one(x)
 
     def finish(who, slot, j):
         landed(xrecv.at[who, slot, j], x_r.at[who, slot, j])
@@ -624,7 +627,7 @@
 
     def store(slot, at):
         where = pl.ds(place_of(slot, at), cols)
-        return pltpu.make_async_copy(out_ref.at[:, where], result_hbm.at[:, where], out_s.at[slot, at])
+        return pltpu.make_async_copy(out_ref.at[:, where], result_hbm.at[:, where], out_s)
 
     def settle(slot, at, start):
         first = pl.multiple_of(place_of(slot, at) + start * cut, 128)
@@ -664,12 +667,25 @@
     lax.fori_loop(0, outer, collect_at, 0)
     lax.fori_loop(0, outer, drain, 0)
 
-    def stored(slot, _):
-        for at in range(inner):
-            store(slot, at).wait()
-        return 0
-
-    lax.fori_loop(0, outer, stored, 0)
+    landed(out_ref, out_s)
+
+
+def hand_over(parts, src, dst, held, in_s, out_s):
+    rows = src.shape[0] // parts
+    moves = []
+    for k in range(parts):
+        at = pl.ds(k * rows, rows)
+        moves.append((
+            pltpu.make_async_copy(src.at[at, :], held.at[at, :], in_s.at[k]),
+            pltpu.make_async_copy(held.at[at, :], dst.at[at, :], out_s.at[k]),
+        ))
+    for take, _ in moves:
+        take.start()
+    for take, give in moves:
+        take.wait()
+        give.start()
+    for _, give in moves:
+        give.wait()
 
 
 def on_device(queries, keys, values, positions, segment_ids, out_weight, residual):
@@ -686,7 +702,7 @@
     block = inner * quarter
     bf16 = jnp.bfloat16
     dma = pltpu.SemaphoreType.DMA
-    return pl.pallas_call(
+    summed = pl.pallas_call(
         functools.partial(fused, n, inner, reach, tile),
         out_shape=jax.ShapeDtypeStruct((quarter, n * cols), bf16),
         in_specs=[pl.BlockSpec(memory_space=pltpu.HBM)] * 8,
@@ -712,7 +728,7 @@
             pltpu.VMEM((2, outer, pieces, 2, block, cut), bf16),
             pltpu.VMEM((2, outer, pieces, block, cut), bf16),
             pltpu.VMEM((2, outer, pieces, inner, quarter, cut), bf16),
-            dma((7,)), dma((outer, inner)),
+            dma((7,)), dma,
             dma((reach // inner + 1, inner) if reach % inner == 0 else (1, reach + 1)), dma((reach, 4)),
             dma((outer, 2, pieces)), dma((outer,)), dma((outer,)), dma((outer,)),
             dma((inner, 2)), dma((inner, 2, 2)),
@@ -724,6 +740,16 @@
             collective_id=0, has_side_effects=True, vmem_limit_bytes=60 * 1024 * 1024
         ),
     )(keys, values, positions, segment_ids[None, :], half_frequencies(), queries, residual, out_weight)
+    parts = math.gcd(quarter // 16, 8)
+    hbm = pl.BlockSpec(memory_space=pltpu.HBM)
+    return pl.pallas_call(
+        functools.partial(hand_over, parts),
+        out_shape=jax.ShapeDtypeStruct(summed.shape, bf16),
+        in_specs=[hbm],
+        out_specs=hbm,
+        scratch_shapes=[pltpu.VMEM(summed.shape, bf16), dma((parts,)), dma((parts,))],
+        compiler_params=pltpu.CompilerParams(vmem_limit_bytes=60 * 1024 * 1024),
+    )(summed)
 
 
 def solution(mesh):

time: 121 us -> 121 us (level)
  local copies, waits for them, and re-layouts: 3.1 us -> 0 us
  Pallas kernels: 117 us -> 120 us
    unnamed x1 -> x0, local copies, waits for them, and re-layouts: 3.1 us -> none
    pallas_call x0 -> x1, Pallas kernels: none -> 2.39 us  [on_device(): pl.pallas_call(functools.partial(hand_over, parts), out_shape=jax.ShapeDt...]
where the time goes in v7:
time: 121 us; the launch traced here: 120 us
  Pallas kernels  120 us (99%)
    pallas_call x1, Pallas kernels, on_device(): pl.pallas_call(functools.partial(fused, n, inner, reach, tile), out_shape...  118 us

profile of v7, /device:TPU:0, one launch (start us, length us, event | category | flops | bytes accessed | tf_op | source)
XLA Modules:
  0.0 120.5 jit_solution(56584125619714836)
XLA Ops:
  0.0 118.1 %shard_map.82.src = bf16[128,8192]{1,0:T(8,128)(2,1)} custom-call(bf16[512,128]{1,0:T(8,128)(2,1)} %k_hbm.1, bf16[512,128]{1,0:T(8,128)(2,1)} %v_hbm.1, s32[3,512]{1,0:T(4,128)} %place_hbm.1, s32[1,4096]{1,0:T(1,128)} %bitcast.1, f32[64,128]{1,0:T(8,128)} %constant.2.clone.freq_hbm, bf16[512,1024]{1,0:T(8,128)(2,1)} %q_hbm.1, ...), custom_call_target="tpu_custom_call" | custom-call | tf_op jit(solution)/shard_map/pallas_call | solution.py:705
  118.1 2.4 %shard_map.83 = bf16[128,8192]{1,0:T(8,128)(2,1)} custom-call(bf16[128,8192]{1,0:T(8,128)(2,1)} %shard_map.82.src), custom_call_target="tpu_custom_call" | custom-call | tf_op jit(solution)/shard_map/pallas_call | solution.py:745
